TPU v7x, 32 devices: a whole 2x2x4 slice. The times are simulated.
32 devices in a mesh: group: 4 (over y, core), freq: 8 (over z, x).
Axes of the slice: x: 2, y: 2, z: 4, core: 2. Of those that a mesh axis runs over, the one named last changes fastest.
Arguments:
- spectra: bfloat16 [2048, 2, 16], P('freq', None, 'group'), may hold values from -6 to 6
- templates: bfloat16 [2048, 2, 2560], P('freq', None, 'group'), may hold values from -600 to 600
- valid_start: int32 [16], replicated, may hold values from 0 to 2048
Outputs:
- peaks: float32 [2560, 16], P('group')
All inputs are finite; a program needn't handle non-finite values.
Results may differ from a plain program's by a relative error of at most 0.0019.
Values may be sent and summed in bfloat16 or wider, within the bound.
No kernel may reach another device: no remote copies, remote signals or barrier semaphores. Data moves between devices by JAX's collectives and lax.ppermute only.
A program may use at most 256 MiB of HBM per device.

v0:
```python
import math

import jax
import jax.numpy as jnp
from jax import lax
from jax.sharding import PartitionSpec as P

N = 4096
VALID = 2048


def make_table(bins_count, lag_index):
    bins_index = jnp.arange(bins_count, dtype=jnp.int32)
    angle = (bins_index[:, None] * lag_index[None, :] % N).astype(jnp.float32) * (2.0 * math.pi / N)
    cosine = jnp.cos(angle)
    sine_part = jnp.sin(angle)
    upper = jnp.concatenate([cosine, sine_part], 1)
    lower = jnp.concatenate([-sine_part, cosine], 1)
    return jnp.concatenate([upper, lower], 0).astype(jnp.bfloat16)


def make_cross(bank_piece, seg_piece):
    bank_re = bank_piece[:, 0, :].astype(jnp.float32)[:, None, :]
    bank_im = bank_piece[:, 1, :].astype(jnp.float32)[:, None, :]
    seg_re = seg_piece[:, 0, :].astype(jnp.float32)[:, :, None]
    seg_im = seg_piece[:, 1, :].astype(jnp.float32)[:, :, None]
    cross_re = bank_re * seg_re + bank_im * seg_im
    cross_im = bank_re * seg_im - bank_im * seg_re
    joined = jnp.stack([cross_re, cross_im], 0).astype(jnp.bfloat16)
    return joined.reshape(2 * joined.shape[1], joined.shape[2] * joined.shape[3])


def contract(cross, table):
    return lax.dot_general(
        cross, table, (((0,), (0,)), ((), ())), preferred_element_type=jnp.float32
    )


def on_device(spectra, templates, valid_start):
    freq_count = lax.axis_size("freq")
    lag_count = N // freq_count
    lag_index = lax.axis_index("freq") * lag_count + jnp.arange(lag_count, dtype=jnp.int32)
    tpl_rows = templates.shape[2]
    every_segment = lax.all_gather(spectra, "group", axis=2, tiled=True)
    count = every_segment.shape[2]
    bank_piece = lax.all_gather(templates, "freq", axis=0, tiled=True)
    seg_piece = lax.all_gather(every_segment, "freq", axis=0, tiled=True)
    width = bank_piece.shape[0]
    cross = make_cross(bank_piece, seg_piece)
    series = contract(cross, make_table(width, lag_index))
    bank_float = bank_piece.astype(jnp.float32)
    norm_sum = jnp.sum(bank_float * bank_float, axis=(0, 1))
    series, template_norm = (series, norm_sum)
    power = (
        series[:, :lag_count] * series[:, :lag_count]
        + series[:, lag_count:] * series[:, lag_count:]
    )
    power = power.reshape(count, tpl_rows, lag_count) / template_norm[None, :, None]
    inside = (lag_index[None, :] >= valid_start[:, None]) & (
        lag_index[None, :] < valid_start[:, None] + VALID
    )
    peaks = jnp.max(jnp.where(inside[:, None, :], power, jnp.float32(0.0)), axis=2).T
    return lax.pmax(peaks, "freq")


def solution(mesh):
    in_specs = (P("freq", None, "group"), P("freq", None, "group"), P())
    out_specs = P("group", None)
    return jax.shard_map(
        on_device, mesh=mesh, in_specs=in_specs, out_specs=out_specs, check_vma=False
    )
```

profile of v0, /device:TPU:0, one launch (start us, length us, event | category | flops | bytes accessed | tf_op | source)
XLA Modules:
  0.0 411.2 jit_solution(10462110616772859024)
XLA Ops:
  6.5 0.0 all-gather.2.cloned.1.call-start
  6.5 2.0 copy.14
  8.5 0.0 all-gather.2.cloned.1.call-update
  8.6 0.7 copy.15
  9.3 6.3 %all_gather.10 = bf16[256,2,16]{0,1,2:T(2,128)(2,1)S(1)} all-gather(bf16[256,2,4]{0,1,2:T(2,128)(2,1)S(1)} %copy.15), channel_id=1, replica_groups=mesh['group'=4,'freq'=8] {'group'}, dimensions={2}, use_global_device_ids=true | all-gather | bytes 20480 | tf_op jit(solution)/shard_map/all_gather | solution.py:44
  15.5 23.8 %all_gather.11 = bf16[2048,2,16]{0,1,2:T(2,128)(2,1)S(1)} all-gather(bf16[256,2,16]{0,1,2:T(2,128)(2,1)S(1)} %all_gather.10), channel_id=1, replica_groups=mesh['group'=4,'freq'=8] {'freq'}, dimensions={0}, use_global_device_ids=true | all-gather | bytes 147456 | tf_op jit(solution)/shard_map/all_gather | solution.py:47
  39.3 0.2 slice_convert_fusion.1
  39.5 0.3 copy.18
  39.9 0.3 copy.19
  40.2 0.7 broadcast_add_fusion
  40.9 0.7 compare_and_fusion
  41.6 0.2 copy.13
  41.8 2.8 broadcast_in_dim.10
  44.6 5.5 %copy.20 = pred[64,8,16,640]{3,1,2,0:T(8,128)(4,1)} copy(pred[64,8,16,640]{3,2,1,0:T(8,128)(4,1)S(1)} %bitcast.22) | data formatting | bytes 10485760
  50.2 18.7 %fusion.21 = (bf16[2048,512]{1,0:T(8,128)(2,1)}, bf16[2048,512]{1,0:T(8,128)(2,1)}, bf16[2048,512]{1,0:T(8,128)(2,1)}) fusion(s32[512]{0:T(512)S(1)} %iota_add_fusion), kind=kLoop, calls=%fused_computation.34 | loop fusion | flops 18874368 | bytes 6293504 | tf_op jit(solution)/shard_map/convert.9
  68.8 30.4 %all-gather.2.cloned.1.call-done = bf16[2048,2,640]{2,0,1:T(8,128)(2,1)} async-done(((bf16[256,2,640]{2,0,1:T(8,128)(2,1)}), bf16[2048,2,640]{2,0,1:T(8,128)(2,1)}) %all-gather.2.cloned.1.call-update) | async-done | bytes 5242896 | tf_op jit(solution)/shard_map/all_gather | solution.py:46
  99.2 7.2 %fusion.19 = (f32[2048,640]{1,0:T(8,128)}, f32[2048,640]{1,0:T(8,128)}) fusion(bf16[2048,2,640]{2,0,1:T(8,128)(2,1)} %all-gather.2.cloned.1.call-done), kind=kLoop, calls=%fused_computation.32 | loop fusion | flops 2621440 | bytes 15728640 | tf_op jit(solution)/shard_map/mul | solution.py:27
  106.4 31.5 %add_convert_fusion = (bf16[1,2048,16,640]{3,2,1,0:T(8,128)(2,1)}, bf16[1,2048,16,640]{3,2,1,0:T(8,128)(2,1)}) fusion(f32[2048,16]{1,0:T(8,128)S(1)} %bitcast.25, f32[2048,640]{1,0:T(8,128)} %get-tuple-element.8, f32[2048,16]{1,0:T(8,128)S(1)} %bitcast.24, f32[2048,640]{1,0:T(8,128)} %get-tuple-element.7), kind=kLoop, calls=%fused_computation.2 | loop fusion | flops 167772160 | bytes 94633984 | tf_op jit(solution)/shard_map/convert.10
  137.9 56.2 %pad_maximum_fusion = bf16[2,2048,16,640]{3,2,1,0:T(8,128)(2,1)} fusion(bf16[1,2048,16,640]{3,2,1,0:T(8,128)(2,1)} %get-tuple-element.6, bf16[1,2048,16,640]{3,2,1,0:T(8,128)(2,1)} %get-tuple-element.5), kind=kLoop, calls=%fused_computation | loop fusion | flops 41943040 | bytes 167772160 | tf_op jit(solution)/shard_map/stack | solution.py:29
  194.1 0.0 copy-start
  194.1 55.4 %copy.21 = bf16[512,8,16,640]{3,1,2,0:T(8,128)(2,1)} copy(bf16[512,8,16,640]{3,2,1,0:T(8,128)(2,1)} %bitcast.12) | data formatting | bytes 167772160
  249.5 3.6 multiply_reduce_fusion
  253.1 0.6 div.14
  253.7 0.0 copy-done
  253.7 0.0 copy-start.1
  253.7 99.3 %fusion.4 = f32[10240,1024]{0,1:T(8,128)} fusion(bf16[4096,10240]{1,0:T(8,128)(2,1)} %bitcast.13, bf16[2048,512]{1,0:T(8,128)(2,1)} %get-tuple-element.13, bf16[2048,512]{1,0:T(8,128)(2,1)} %get-tuple-element.12, bf16[2048,512]{1,0:T(8,128)(2,1)S(1)} %copy-done), kind=kOutput, calls=%fused_computation.10 | convolution fusion | flops 85932900352 | bytes 132120576 | tf_op jit(solution)/shard_map/dot_general | solution.py:34
  353.0 0.0 copy-done.1
  353.0 15.9 %fusion.3 = f32[10240]{0:T(1024)S(1)} fusion(pred[10240,512]{0,1:T(8,128)(4,1)} %bitcast.23, f32[10240,1024]{0,1:T(8,128)} %fusion.4, f32[10240]{0:T(1024)S(1)} %copy-done.1), kind=kLoop, calls=%fused_computation.8 | loop fusion | flops 31447040 | bytes 47267840 | tf_op jit(solution)/shard_map/reduce_max | solution.py:62
  369.0 35.3 %pmax.7 = f32[640,16]{0,1:T(8,128)} all-reduce(f32[640,16]{0,1:T(8,128)S(1)} %bitcast.26), channel_id=1, replica_groups=mesh['group'=4,'freq'=8] {'freq'}, use_global_device_ids=true, to_apply=%region_2.3 | all-reduce | flops 10240 | bytes 81920 | tf_op jit(solution)/shard_map/pmax | solution.py:63
  (3 shorter events, 0.0 us)
Async XLA Ops:
  6.5 92.7 %all-gather.2.cloned.1.call-start = ((), (), s32[]{:S(2)}) async-start(), calls=%async_computation | async-start | bytes 5898240 | tf_op jit(solution)/shard_map/all_gather | solution.py:46
  194.1 59.7 %copy-start = (bf16[2048,512]{1,0:T(8,128)(2,1)S(1)}, bf16[2048,512]{1,0:T(8,128)(2,1)}, u32[]{:S(2)}) copy-start(bf16[2048,512]{1,0:T(8,128)(2,1)} %get-tuple-element.11) | copy-start | bytes 6291460
  253.7 99.3 %copy-start.1 = (f32[10240]{0:T(1024)S(1)}, f32[10240]{0:T(1024)}, u32[]{:S(2)}) copy-start(f32[10240]{0:T(1024)} %div.14) | copy-start | bytes 122884
Sparse Core Ops, SparseCore 0:
  9.5 89.6 all-gather.1
where the time goes:
time: 411 us
  other arithmetic  135 us (33%)
  matrix products  99.3 us (24%)
  local copies, waits for them, and re-layouts  68 us (17%)
  blocking collectives  65.4 us (16%)
  waiting for transfers between devices  30.4 us (7%)
  between operations  13.5 us (3%)
    dot_general x1, matrix products, contract(): lax.dot_general(cross, table, (((0,), (0,)), ((), ())), preferred_element...  99.3 us
    unnamed x8, local copies, waits for them, and re-layouts  63.7 us
    another operation x1, other arithmetic, make_cross(): joined = jnp.stack([cross_re, cross_im], 0).astype(jnp.bfloat16)  56.2 us
    another operation x2, other arithmetic  50.2 us
    pmax x1, blocking collectives, on_device(): return lax.pmax(peaks, 'freq')  35.3 us
    all_gather x1, waiting for transfers between devices, on_device(): bank_piece = lax.all_gather(templates, 'freq', axis=0, tiled=True)  30.4 us
    all_gather x1, blocking collectives, on_device(): seg_piece = lax.all_gather(every_segment, 'freq', axis=0, tiled=True)  23.8 us
    reduce_max x1, other arithmetic, on_device(): jnp.max(jnp.where(inside[:, None, :], power, jnp.float32(0.0)), axis=2)  15.9 us
  transfers between devices with their start and end apart: 1, of which 1 were waited for; matrix products, arithmetic and copies ran while one was open for 7% of the time, Pallas kernels for 0%

commit v1 on v0

v1 whole, which is shorter than its diff:
```python
import math

import jax
import jax.numpy as jnp
import numpy as np
from jax import lax
from jax.experimental import pallas as pl
from jax.experimental.pallas import tpu as pltpu
from jax.sharding import PartitionSpec as P

N = 4096
VALID = 2048
RADIX = 8
LANES = 128


def twiddles(bins):
    span = N // RADIX
    rows = bins // RADIX // 16
    t1 = np.arange(span)[None, :]
    fine = 2.0 * math.pi * ((np.arange(16)[:, None] * t1) % span) / span
    coarse = 2.0 * math.pi * ((16 * np.arange(rows)[:, None] * t1) % span) / span
    low = 2.0 * math.pi * ((np.arange(RADIX)[:, None] * t1) % N) / N
    both = lambda angle: np.stack([np.cos(angle), np.sin(angle)]).astype(np.float32)
    return both(fine), both(coarse).swapaxes(0, 1), both(low)


def transform(recv, valid_start, tpl_count):
    sources, rows_all, local = recv.shape
    segs = rows_all - tpl_count
    piece = local // (2 * RADIX)
    per_class = sources * piece
    bins = per_class * RADIX
    span = N // RADIX
    half = span // 2
    tpl_pad = -(-tpl_count // 16) * 16
    block_segs = max(d for d in range(1, segs + 1) if segs % (2 * d) == 0 and (d == 1 or d * tpl_pad <= 400))
    blocks = segs // block_segs
    rows = block_segs * tpl_pad
    tiles = per_class // LANES
    fine, coarse, low = twiddles(bins)
    pad = tpl_pad - tpl_count
    if pad:
        recv = jnp.concatenate(
            [recv[:, :tpl_count], jnp.zeros((sources, pad, local), recv.dtype), recv[:, tpl_count:]], 1
        )
    rows_all = tpl_pad + segs
    root = np.float32(math.sqrt(0.5))

    def kernel(start_ref, recv_ref, fine_ref, coarse_ref, low_ref, out_ref, wide, strain, table, xa, xb, ya, yb, acc):
        def table_rows(a, carry):
            cr = coarse_ref[a, 0:1, :]
            ci = coarse_ref[a, 1:2, :]
            ar = cr * fine_ref[0] - ci * fine_ref[1]
            ai = cr * fine_ref[1] + ci * fine_ref[0]
            at = pl.multiple_of(a * 16, 16)
            for k2 in range(RADIX):
                lr = low_ref[0, k2 : k2 + 1, :]
                li = low_ref[1, k2 : k2 + 1, :]
                c = ar * lr - ai * li
                s = ar * li + ai * lr
                cb = c.astype(jnp.bfloat16)
                sb = s.astype(jnp.bfloat16)
                nb = (-s).astype(jnp.bfloat16)
                for ph in range(2):
                    col = ph * span
                    t = slice(ph * half, (ph + 1) * half)
                    table[k2, pl.ds(at, 16), col : col + half] = cb[:, t]
                    table[k2, pl.ds(at, 16), col + half : col + span] = sb[:, t]
                    table[k2, pl.ds(per_class + at, 16), col : col + half] = nb[:, t]
                    table[k2, pl.ds(per_class + at, 16), col + half : col + span] = cb[:, t]
            return carry

        lax.fori_loop(0, per_class // 16, table_rows, 0)

        lane = lax.broadcasted_iota(jnp.int32, (rows_all, LANES), 1)
        per_tile = LANES // piece
        for k2 in range(RADIX):
            for c in range(2):
                lane0 = k2 * 2 * piece + c * piece
                tile, inner = lane0 // LANES, lane0 % LANES
                for j in range(tiles):
                    value = None
                    for i in range(per_tile):
                        part = recv_ref[j * per_tile + i, :, tile * LANES : (tile + 1) * LANES].astype(jnp.float32)
                        shift = (i * piece - inner) % LANES
                        if shift:
                            part = pltpu.roll(part, shift, 1)
                        value = part if value is None else jnp.where(lane >= i * piece, part, value)
                    at = k2 * per_class + j * LANES
                    wide[c, :, at : at + LANES] = value

        for s in range(segs):
            for c in range(2):
                strain[s, c : c + 1, :] = wide[c, tpl_pad + s : tpl_pad + s + 1, :]

        def cross_piece(x_ref, block, index):
            tile, i = index // block_segs, index % block_segs
            k2, j = tile // tiles, tile % tiles
            at = slice(tile * LANES, (tile + 1) * LANES)
            seg = block * block_segs + i
            d0 = strain[seg, 0:1, at]
            d1 = strain[seg, 1:2, at]
            col = k2 * 2 * per_class + j * LANES
            for t in range(0, tpl_pad, 16):
                h0 = wide[0, t : t + 16, at]
                h1 = wide[1, t : t + 16, at]
                row = slice(i * tpl_pad + t, i * tpl_pad + t + 16)
                x_ref[row, col : col + LANES] = (h0 * d0 + h1 * d1).astype(jnp.bfloat16)
                col_im = col + per_class
                x_ref[row, col_im : col_im + LANES] = (h0 * d1 - h1 * d0).astype(jnp.bfloat16)

        cross_count = RADIX * tiles * block_segs
        lane16 = lax.broadcasted_iota(jnp.int32, (16, LANES), 1)
        lane_tiles = half // LANES
        row_tiles = tpl_pad // 16
        peak_count = block_segs * lane_tiles * row_tiles
        signs = {}

        def peak_piece(y_ref, block, phase, index, key):
            i = index // (lane_tiles * row_tiles)
            u = index // row_tiles % lane_tiles
            r = index % row_tiles
            if (key, i, u) not in signs:
                first = start_ref[block * block_segs + i] - (phase * half + u * LANES)
                one = [jnp.float32(1.0), root, jnp.float32(1.0), root]
                signs[key, i, u] = [
                    jnp.where(lane16 >= first - span * j, one[j], -one[j]) for j in range(4)
                ]
            sign = signs[key, i, u]
            row = slice(i * tpl_pad + r * 16, i * tpl_pad + r * 16 + 16)
            re = lambda k: y_ref[k, row, u * LANES : (u + 1) * LANES]
            im = lambda k: y_ref[k, row, half + u * LANES : half + (u + 1) * LANES]

            def four(a, b, c, d):
                ar, ai, br, bi, cr, ci, dr, di = re(a), im(a), re(b), im(b), re(c), im(c), re(d), im(d)
                pr, pi, qr, qi = ar + cr, ai + ci, ar - cr, ai - ci
                sr, si, wr, wi = br + dr, bi + di, br - dr, bi - di
                return (
                    (pr + sr, pi + si),
                    (qr - wi, qi + wr),
                    (pr - sr, pi - si),
                    (qr + wi, qi - wr),
                )

            even = four(0, 2, 4, 6)
            odd = four(1, 3, 5, 7)
            odd = (
                odd[0],
                (odd[1][0] - odd[1][1], odd[1][0] + odd[1][1]),
                (-odd[2][1], odd[2][0]),
                (-odd[3][0] - odd[3][1], odd[3][0] - odd[3][1]),
            )
            best = None
            for j in range(4):
                yr = even[j][0] + sign[j] * odd[j][0]
                yi = even[j][1] + sign[j] * odd[j][1]
                power = yr * yr + yi * yi
                best = power if best is None else jnp.maximum(best, power)
            if phase == 0 and u == 0:
                acc[block, row, :] = best
            else:
                acc[block, row, :] = jnp.maximum(acc[block, row, :], best)

        for index in range(cross_count):
            cross_piece(xa, 0, index)

        def phase_step(x_ref, y_new, phase, y_old, old_block, old_phase, x_next, next_block, key):
            share_p = -(-peak_count // RADIX)
            share_c = -(-(cross_count // 2) // RADIX)
            for k2 in range(RADIX):
                y_new[k2] = jnp.dot(
                    x_ref[:, k2 * 2 * per_class : (k2 + 1) * 2 * per_class],
                    table[k2, :, phase * span : (phase + 1) * span],
                    preferred_element_type=jnp.float32,
                )
                for index in range(k2 * share_p, min((k2 + 1) * share_p, peak_count)):
                    peak_piece(y_old, old_block, old_phase, index, key)
                for index in range(k2 * share_c, min((k2 + 1) * share_c, cross_count // 2)):
                    cross_piece(x_next, next_block, phase * (cross_count // 2) + index)

        def pair(p, carry):
            signs.clear()
            b = 2 * p
            last = jnp.where(p == 0, blocks, b - 1)
            after = jnp.where(b + 2 < blocks, b + 2, 0)
            phase_step(xa, ya, 0, yb, last, 1, xb, b + 1, 0)
            phase_step(xa, yb, 1, ya, b, 0, xb, b + 1, 1)
            phase_step(xb, ya, 0, yb, b, 1, xa, after, 2)
            phase_step(xb, yb, 1, ya, b + 1, 0, xa, after, 3)
            return carry

        lax.fori_loop(0, blocks // 2, pair, 0)
        signs.clear()
        for index in range(peak_count):
            peak_piece(yb, blocks - 1, 1, index, 0)

        square = wide[0, :tpl_pad, :] * wide[0, :tpl_pad, :] + wide[1, :tpl_pad, :] * wide[1, :tpl_pad, :]
        norm = jnp.sum(square, axis=1, keepdims=True)
        column = lax.broadcasted_iota(jnp.int32, (tpl_pad, segs), 1)
        result = jnp.zeros((tpl_pad, segs), jnp.float32)
        for s in range(segs):
            b, i = s // block_segs, s % block_segs
            top = jnp.max(acc[b, i * tpl_pad : (i + 1) * tpl_pad, :], axis=1, keepdims=True)
            result = jnp.where(column == s, top, result)
        out_ref[...] = result / norm

    any_vmem = pl.BlockSpec(memory_space=pltpu.VMEM)
    peaks = pl.pallas_call(
        kernel,
        out_shape=jax.ShapeDtypeStruct((tpl_pad, segs), jnp.float32),
        in_specs=[pl.BlockSpec(memory_space=pltpu.SMEM)] + [any_vmem] * 4,
        out_specs=any_vmem,
        scratch_shapes=[
            pltpu.VMEM((2, rows_all, bins), jnp.float32),
            pltpu.VMEM((segs, 2, bins), jnp.float32),
            pltpu.VMEM((RADIX, 2 * per_class, 2 * span), jnp.bfloat16),
            pltpu.VMEM((rows, 2 * bins), jnp.bfloat16),
            pltpu.VMEM((rows, 2 * bins), jnp.bfloat16),
            pltpu.VMEM((RADIX, rows, span), jnp.float32),
            pltpu.VMEM((RADIX, rows, span), jnp.float32),
            pltpu.VMEM((blocks + 1, rows, LANES), jnp.float32),
        ],
        compiler_params=pltpu.CompilerParams(vmem_limit_bytes=48 * 1024 * 1024),
        name="transform",
    )(valid_start, recv, jnp.asarray(fine), jnp.asarray(coarse), jnp.asarray(low))
    return peaks[:tpl_count]


def by_class(array):
    bins, two, columns = array.shape
    split = array.reshape(bins // RADIX, RADIX, two, columns)
    return split.transpose(3, 1, 2, 0).reshape(columns, two * bins)


def spread(block, axis):
    count = lax.axis_size(axis)
    index = lax.axis_index(axis)
    step = 1
    while step < count:
        other = lax.ppermute(block, axis, [(j, j ^ step) for j in range(count)])
        low = jnp.concatenate([block, other], 0)
        high = jnp.concatenate([other, block], 0)
        block = jnp.where((index & step) == 0, low, high)
        step *= 2
    return block


def on_device(spectra, templates, valid_start):
    freq_count = lax.axis_size("freq")
    tpl_count = templates.shape[2] // freq_count
    segments = lax.all_gather(by_class(spectra), "group", axis=0, tiled=True)
    bank = by_class(templates).reshape(freq_count, tpl_count, -1)
    every = jnp.broadcast_to(segments[None], (freq_count,) + segments.shape)
    recv = lax.all_to_all(jnp.concatenate([bank, every], 1), "freq", 0, 0, tiled=True)
    peaks = transform(recv, valid_start, tpl_count)
    return spread(peaks, "freq")


def solution(mesh):
    in_specs = (P("freq", None, "group"), P("freq", None, "group"), P())
    out_specs = P("group", None)
    return jax.shard_map(
        on_device, mesh=mesh, in_specs=in_specs, out_specs=out_specs, check_vma=False
    )
```

time: 411 us -> 72.6 us (0.18)
  other arithmetic: 135 us -> 0.91 us
  matrix products: 99.3 us -> 0 us
  local copies, waits for them, and re-layouts: 68 us -> 3.42 us
  blocking collectives: 65.4 us -> 33 us
  Pallas kernels: 0 us -> 22.4 us
  waiting for transfers between devices: 30.4 us -> 8.84 us
  between operations: 13.5 us -> 0.11 us
    another operation x3 -> x0, other arithmetic: 106 us -> none  [the longest x1 56.2 us: make_cross(): joined = jnp.stack([cross_re, cross_im], 0).astype(jnp.bfloat16)]
    dot_general x1 -> x0, matrix products: 99.3 us -> none  [contract(): lax.dot_general(cross, table, (((0,), (0,)), ((), ())), preferred_element...]
    unnamed x8 -> x12, local copies, waits for them, and re-layouts: 63.7 us -> 0.14 us
    pmax x1 -> x0, blocking collectives: 35.3 us -> none  [on_device(): return lax.pmax(peaks, 'freq')]
    all_gather x1 -> x0, waiting for transfers between devices: 30.4 us -> none  [on_device(): bank_piece = lax.all_gather(templates, 'freq', axis=0, tiled=True)]
    all_to_all x0 -> x1, blocking collectives: none -> 26.8 us  [on_device(): lax.all_to_all(jnp.concatenate([bank, every], 1), 'freq', 0, 0, tiled=True)]
    all_gather x2 -> x1, blocking collectives: 30.1 us -> 6.26 us  [on_device(): segments = lax.all_gather(by_class(spectra), 'group', axis=0, tiled=True)]
    pallas_call x0 -> x1, Pallas kernels: none -> 22.4 us  [transform(): pl.pallas_call(kernel, out_shape=jax.ShapeDtypeStruct((tpl_pad, segs), jn...]
  transfers between devices with their start and end apart: 1 -> 3, of which waited for: 1 -> 3; matrix products, arithmetic and copies ran while one was open for 7% -> 0% of each run, Pallas kernels for 0% -> 0%
where the time goes in v1:
time: 72.6 us; the launch traced here: 72.3 us
  blocking collectives  33 us (45%)
  Pallas kernels  22.4 us (31%)
  waiting for transfers between devices  8.84 us (12%)
  starting transfers between devices  3.61 us (5%)
  local copies, waits for them, and re-layouts  3.42 us (5%)
  other arithmetic  0.91 us (1%)
    all_to_all x1, blocking collectives, on_device(): lax.all_to_all(jnp.concatenate([bank, every], 1), 'freq', 0, 0, tiled=True)  26.8 us
    pallas_call x1, Pallas kernels, transform(): pl.pallas_call(kernel, out_shape=jax.ShapeDtypeStruct((tpl_pad, segs), jn...  22.4 us
    ppermute x3, waiting for transfers between devices, spread(): other = lax.ppermute(block, axis, [(j, j ^ step) for j in range(count)])  8.84 us
    all_gather x1, blocking collectives, on_device(): segments = lax.all_gather(by_class(spectra), 'group', axis=0, tiled=True)  6.26 us
    ppermute x3, starting transfers between devices, spread(): other = lax.ppermute(block, axis, [(j, j ^ step) for j in range(count)])  3.61 us
    another operation x2, local copies, waits for them, and re-layouts, on_device(): bank = by_class(templates).reshape(freq_count, tpl_count, -1)  1.74 us
  transfers between devices with their start and end apart: 3, of which 3 were waited for; matrix products, arithmetic and copies ran while one was open for 0% of the time, Pallas kernels for 0%

profile of v1, /device:TPU:0, one launch (start us, length us, event | category | flops | bytes accessed | tf_op | source)
XLA Modules:
  0.0 72.3 jit_solution(16315640434777077254)
XLA Ops:
  0.0 1.2 %copy.21 = bf16[32,8,2,640]{3,0,2,1:T(8,128)(2,1)S(1)} copy(bf16[32,8,2,640]{3,2,1,0:T(2,128)(2,1)} %bitcast.12) | data formatting | bytes 1310720 | tf_op jit(solution)/shard_map/reshape | solution.py:232
  1.2 1.0 %reshape_reshape.3 = bf16[8,80,512]{1,0,2:T(8,128)(2,1)S(1)} reshape(bf16[640,8,2,32]{0,3,2,1:T(8,128)(2,1)S(1)} %bitcast.11) | data formatting | bytes 1310720 | tf_op jit(solution)/shard_map/reshape;reshape | solution.py:253
  2.3 0.0 copy-start.4
  2.3 0.7 copy.15
  3.0 0.0 copy-done.4
  3.0 0.1 reshape.11
  3.1 0.1 copy.14
  3.2 0.1 reshape.13
  3.3 6.3 %all-gather = bf16[4,4,512]{2,1,0:T(4,128)(2,1)S(1)} all-gather(bf16[1,4,512]{2,1,0:T(4,128)(2,1)S(1)} %reshape.13), channel_id=1, replica_groups=mesh['group'=4,'freq'=8] {'group'}, dimensions={0}, use_global_device_ids=true | all-gather | bytes 20480 | tf_op jit(solution)/shard_map/all_gather | solution.py:252
  9.6 0.1 pad_maximum_fusion
  9.7 0.0 copy-start
  9.7 0.0 copy-start.1
  9.7 0.0 copy-start.2
  9.7 0.0 copy-start.3
  9.7 26.8 %all_to_all.5.recv_ref = bf16[8,96,512]{2,1,0:T(8,128)(2,1)S(1)} all-to-all(bf16[8,96,512]{2,1,0:T(8,128)(2,1)S(1)} %pad_maximum_fusion), channel_id=1, replica_groups=mesh['group'=4,'freq'=8] {'freq'}, dimensions={0} | all-to-all | bytes 1572864 | tf_op jit(solution)/shard_map/all_to_all | solution.py:255
  36.5 0.0 copy-done
  36.5 0.0 copy-done.1
  36.5 0.0 copy-done.2
  36.5 0.0 copy-done.3
  36.5 22.4 %transform.1 = f32[80,16]{1,0:T(8,128)S(1)} custom-call(s32[16]{0:T(128)S(1)} %copy-done.3, bf16[8,96,512]{2,1,0:T(8,128)(2,1)S(1)} %all_to_all.5.recv_ref, f32[2,16,512]{2,1,0:T(8,128)S(1)} %copy-done, f32[16,2,512]{2,1,0:T(2,128)S(1)} %copy-done.1, f32[2,8,512]{2,1,0:T(8,128)S(1)} %copy-done.2), custom_call_target="tpu_custom_call" | custom-call | tf_op jit(solution)/shard_map/transform/pallas_call | solution.py:209
  58.9 1.5 %collective-permute-start = (f32[80,16]{1,0:T(8,128)S(1)}, f32[80,16]{1,0:T(8,128)S(1)}, u32[]{:S(2)}, u32[]{:S(2)}) collective-permute-start(f32[80,16]{1,0:T(8,128)S(1)} %transform.1), channel_id=1, source_target_pairs={{0,1},{1,0},{2,3},{3,2},{4,5},{5,4},{6,7},{7,6},{8,9},{9,8},{10,11... | collective-permute-start | bytes 15368 | tf_op jit(solution)/shard_map/ppermute | solution.py:241
  60.4 0.1 copy.16
  60.4 2.5 %collective-permute-done = f32[80,16]{1,0:T(8,128)S(1)} collective-permute-done((f32[80,16]{1,0:T(8,128)S(1)}, f32[80,16]{1,0:T(8,128)S(1)}, u32[]{:S(2)}, u32[]{:S(2)}) %collective-permute-start) | collective-permute-done | bytes 5152 | tf_op jit(solution)/shard_map/ppermute | solution.py:241
  62.9 0.1 copy.17
  63.0 0.1 maximum_select_fusion.2
  63.0 1.2 %collective-permute-start.1 = (f32[160,16]{0,1:T(8,128)S(1)}, f32[160,16]{0,1:T(8,128)S(1)}, u32[]{:S(2)}, u32[]{:S(2)}) collective-permute-start(f32[160,16]{0,1:T(8,128)S(1)} %maximum_select_fusion.2), channel_id=1, source_target_pairs={{0,2},{1,3},{2,0},{3,1},{4,6},{5,7},{6,4},{7,5},{8,10},{9,11},{10,... | collective-permute-start | bytes 30728 | tf_op jit(solution)/shard_map/ppermute | solution.py:241
  64.2 2.6 %collective-permute-done.1 = f32[160,16]{0,1:T(8,128)S(1)} collective-permute-done((f32[160,16]{0,1:T(8,128)S(1)}, f32[160,16]{0,1:T(8,128)S(1)}, u32[]{:S(2)}, u32[]{:S(2)}) %collective-permute-start.1) | collective-permute-done | bytes 10272 | tf_op jit(solution)/shard_map/ppermute | solution.py:241
  66.8 0.1 maximum_select_fusion.1
  66.9 1.0 %collective-permute-start.2 = (f32[320,16]{0,1:T(8,128)S(1)}, f32[320,16]{0,1:T(8,128)S(1)}, u32[]{:S(2)}, u32[]{:S(2)}) collective-permute-start(f32[320,16]{0,1:T(8,128)S(1)} %maximum_select_fusion.1), channel_id=1, source_target_pairs={{0,4},{1,5},{2,6},{3,7},{4,0},{5,1},{6,2},{7,3},{8,12},{9,13},{10,... | collective-permute-start | bytes 61448 | tf_op jit(solution)/shard_map/ppermute | solution.py:241
  67.9 3.8 %collective-permute-done.2 = f32[320,16]{0,1:T(8,128)S(1)} collective-permute-done((f32[320,16]{0,1:T(8,128)S(1)}, f32[320,16]{0,1:T(8,128)S(1)}, u32[]{:S(2)}, u32[]{:S(2)}) %collective-permute-start.2) | collective-permute-done | bytes 20512 | tf_op jit(solution)/shard_map/ppermute | solution.py:241
  71.6 0.7 maximum_select_fusion
  (2 shorter events, 0.0 us)
Async XLA Ops:
  2.3 0.7 copy-start.4
  9.7 26.8 %copy-start = (f32[2,16,512]{2,1,0:T(8,128)S(1)}, f32[2,16,512]{2,1,0:T(8,128)}, u32[]{:S(2)}) copy-start(f32[2,16,512]{2,1,0:T(8,128)} %constant.18.clone.fine_ref) | copy-start | bytes 196612
  9.7 26.8 %copy-start.1 = (f32[16,2,512]{2,1,0:T(2,128)S(1)}, f32[16,2,512]{2,1,0:T(2,128)}, u32[]{:S(2)}) copy-start(f32[16,2,512]{2,1,0:T(2,128)} %constant.19.clone.coarse_ref) | copy-start | bytes 196612
  9.7 26.8 %copy-start.2 = (f32[2,8,512]{2,1,0:T(8,128)S(1)}, f32[2,8,512]{2,1,0:T(8,128)}, u32[]{:S(2)}) copy-start(f32[2,8,512]{2,1,0:T(8,128)} %constant.20.clone.low_ref) | copy-start | bytes 98308
  9.7 26.8 %copy-start.3 = (s32[16]{0:T(128)S(1)}, s32[16]{0:T(128)}, u32[]{:S(2)}) copy-start(s32[16]{0:T(128)} %start_ref.1) | copy-start | bytes 196
  58.9 4.0 %collective-permute-start = (f32[80,16]{1,0:T(8,128)S(1)}, f32[80,16]{1,0:T(8,128)S(1)}, u32[]{:S(2)}, u32[]{:S(2)}) collective-permute-start(f32[80,16]{1,0:T(8,128)S(1)} %transform.1), channel_id=1, source_target_pairs={{0,1},{1,0},{2,3},{3,2},{4,5},{5,4},{6,7},{7,6},{8,9},{9,8},{10,11... | collective-permute-start | bytes 15368 | tf_op jit(solution)/shard_map/ppermute | solution.py:241
  63.0 3.8 %collective-permute-start.1 = (f32[160,16]{0,1:T(8,128)S(1)}, f32[160,16]{0,1:T(8,128)S(1)}, u32[]{:S(2)}, u32[]{:S(2)}) collective-permute-start(f32[160,16]{0,1:T(8,128)S(1)} %maximum_select_fusion.2), channel_id=1, source_target_pairs={{0,2},{1,3},{2,0},{3,1},{4,6},{5,7},{6,4},{7,5},{8,10},{9,11},{10,... | collective-permute-start | bytes 30728 | tf_op jit(solution)/shard_map/ppermute | solution.py:241
  66.9 4.7 %collective-permute-start.2 = (f32[320,16]{0,1:T(8,128)S(1)}, f32[320,16]{0,1:T(8,128)S(1)}, u32[]{:S(2)}, u32[]{:S(2)}) collective-permute-start(f32[320,16]{0,1:T(8,128)S(1)} %maximum_select_fusion.1), channel_id=1, source_target_pairs={{0,4},{1,5},{2,6},{3,7},{4,0},{5,1},{6,2},{7,3},{8,12},{9,13},{10,... | collective-permute-start | bytes 61448 | tf_op jit(solution)/shard_map/ppermute | solution.py:241

commit v2 on v1

v2 whole, which is shorter than its diff:
```python
import math

import jax
import jax.numpy as jnp
import numpy as np
from jax import lax
from jax.experimental import pallas as pl
from jax.experimental.pallas import tpu as pltpu
from jax.sharding import PartitionSpec as P


N = 4096
RADIX = 8
LANES = 128
VMEM_MIB = 52


def twiddles(bins):
    span = N // RADIX
    rows = bins // RADIX // 16
    t1 = np.arange(span)[None, :]
    fine = (np.arange(16)[:, None] * t1) % span / span
    coarse = (16 * np.arange(rows)[:, None] * t1) % span / span
    low = (np.arange(RADIX)[:, None] * t1) % N / N
    angle = 2.0 * math.pi * np.concatenate([fine, low, coarse], 0)
    return np.stack([np.cos(angle), np.sin(angle)], 1).astype(np.float32)


def make_table(bins):
    per_class = bins // RADIX
    span = N // RADIX
    half = span // 2

    def kernel(factor_ref, table, fine):
        for row in range(16):
            for c in range(2):
                fine[c, row : row + 1, :] = factor_ref[row, c : c + 1, :]

        def table_rows(a, carry):
            cr = factor_ref[16 + RADIX + a, 0:1, :]
            ci = factor_ref[16 + RADIX + a, 1:2, :]
            ar = cr * fine[0] - ci * fine[1]
            ai = cr * fine[1] + ci * fine[0]
            at = pl.multiple_of(a * 16, 16)
            for k2 in range(RADIX):
                lr = factor_ref[16 + k2, 0:1, :]
                li = factor_ref[16 + k2, 1:2, :]
                c = (ar * lr - ai * li).astype(jnp.bfloat16)
                s = (ar * li + ai * lr).astype(jnp.bfloat16)
                for ph in range(2):
                    t = slice(ph * half, (ph + 1) * half)
                    table[ph, k2, pl.ds(at, 16), :half] = c[:, t]
                    table[ph, k2, pl.ds(at, 16), half:] = s[:, t]
                    table[ph, k2, pl.ds(per_class + at, 16), :half] = -s[:, t]
                    table[ph, k2, pl.ds(per_class + at, 16), half:] = c[:, t]
            return carry

        lax.fori_loop(0, per_class // 16, table_rows, 0)

    any_vmem = pl.BlockSpec(memory_space=pltpu.VMEM)
    return pl.pallas_call(
        kernel,
        out_shape=jax.ShapeDtypeStruct((2, RADIX, 2 * per_class, span), jnp.bfloat16),
        in_specs=[any_vmem],
        out_specs=any_vmem,
        scratch_shapes=[pltpu.VMEM((2, 16, span), jnp.float32)],
        compiler_params=pltpu.CompilerParams(vmem_limit_bytes=24 * 1024 * 1024),
        name="table",
    )(jnp.asarray(twiddles(bins)))


def transform(bank, strain, place, table, valid_start):
    sources, tpl_count, local = bank.shape
    segs = strain.shape[1]
    piece = local // (2 * RADIX)
    per_class = sources * piece
    bins = per_class * RADIX
    span = N // RADIX
    half = span // 2
    tpl_pad = -(-tpl_count // 16) * 16
    block_segs = max(d for d in range(1, segs + 1) if segs % (2 * d) == 0 and (d == 1 or d * tpl_pad <= 400))
    blocks = segs // block_segs
    rows = block_segs * tpl_pad
    tiles = per_class // LANES
    if tpl_pad > tpl_count:
        bank = jnp.pad(bank, ((0, 0), (0, tpl_pad - tpl_count), (0, 0)))
    root = np.float32(math.sqrt(0.5))

    def kernel(start_hbm, bank_ref, strain_ref, table_ref, out_ref, start_ref, start_sem, table, sem, wide, lines, flat, xa, xb, ya, yb, acc):
        load = pltpu.make_async_copy(table_ref, table, sem)
        load.start()
        fetch = pltpu.make_async_copy(start_hbm, start_ref, start_sem)
        fetch.start()

        def gather(source_ref, at_of, count, store):
            lane = lax.broadcasted_iota(jnp.int32, (count, LANES), 1)
            per_tile = LANES // piece
            for j in range(tiles):
                for q in range(local // LANES):
                    parts = [
                        source_ref[at_of[j * per_tile + i], :, q * LANES : (q + 1) * LANES].astype(jnp.float32)
                        for i in range(per_tile)
                    ]
                    for inner in range(0, LANES, piece):
                        value = None
                        for i in range(per_tile):
                            shift = (i * piece - inner) % LANES
                            part = pltpu.roll(parts[i], shift, 1) if shift else parts[i]
                            value = part if value is None else jnp.where(lane >= i * piece, part, value)
                        k2, c = divmod((q * LANES + inner) // piece, 2)
                        store(c, slice(k2 * per_class + j * LANES, k2 * per_class + (j + 1) * LANES), value)

        def store_bank(c, at, value):
            wide[c, :, at] = value

        def store_lines(c, at, value):
            flat[c, :, at] = value

        gather(bank_ref, range(sources), tpl_pad, store_bank)
        gather(strain_ref, place, segs, store_lines)
        for s in range(segs):
            for c in range(2):
                lines[s, c : c + 1, :] = flat[c, s : s + 1, :]

        def cross_piece(x_ref, block, tile):
            k2, j = tile // tiles, tile % tiles
            at = slice(tile * LANES, (tile + 1) * LANES)
            col = k2 * 2 * per_class + j * LANES
            col_im = col + per_class
            d = [
                [jnp.broadcast_to(lines[block * block_segs + i, c : c + 1, at], (8, LANES)) for c in range(2)]
                for i in range(block_segs)
            ]
            for t in range(0, tpl_pad, 8):
                h0 = wide[0, t : t + 8, at]
                h1 = wide[1, t : t + 8, at]
                for i in range(block_segs):
                    row = slice(i * tpl_pad + t, i * tpl_pad + t + 8)
                    x_ref[row, col : col + LANES] = h0 * d[i][0] + h1 * d[i][1]
                    x_ref[row, col_im : col_im + LANES] = h0 * d[i][1] - h1 * d[i][0]

        cross_count = RADIX * tiles
        lane8 = lax.broadcasted_iota(jnp.int32, (8, LANES), 1)
        lane_tiles = half // LANES
        row_tiles = tpl_pad // 8
        peak_count = block_segs * lane_tiles * row_tiles
        signs = {}

        def peak_piece(y_ref, block, phase, index, key):
            i = index // (lane_tiles * row_tiles)
            u = index // row_tiles % lane_tiles
            r = index % row_tiles
            if (key, i, u) not in signs:
                first = start_ref[block * block_segs + i] - (phase * half + u * LANES)
                one = [jnp.float32(1.0), root, jnp.float32(1.0), root]
                signs[key, i, u] = [
                    jnp.where(lane8 >= first - span * j, one[j], -one[j]) for j in range(4)
                ]
            sign = signs[key, i, u]
            row = slice(i * tpl_pad + r * 8, i * tpl_pad + r * 8 + 8)
            re = lambda k: y_ref[k, row, u * LANES : (u + 1) * LANES]
            im = lambda k: y_ref[k, row, half + u * LANES : half + (u + 1) * LANES]

            def four(a, b, c, d):
                ar, ai, br, bi, cr, ci, dr, di = re(a), im(a), re(b), im(b), re(c), im(c), re(d), im(d)
                pr, pi, qr, qi = ar + cr, ai + ci, ar - cr, ai - ci
                sr, si, wr, wi = br + dr, bi + di, br - dr, bi - di
                return (
                    (pr + sr, pi + si),
                    (qr - wi, qi + wr),
                    (pr - sr, pi - si),
                    (qr + wi, qi - wr),
                )

            even = four(0, 2, 4, 6)
            odd = four(1, 3, 5, 7)
            best = None
            for j in range(4):
                er, ei = even[j]
                (a, b), g = odd[j], sign[j]
                if j == 0:
                    yr, yi = er + g * a, ei + g * b
                elif j == 1:
                    yr, yi = er + g * (a - b), ei + g * (a + b)
                elif j == 2:
                    yr, yi = er - g * b, ei + g * a
                else:
                    yr, yi = er - g * (a + b), ei + g * (a - b)
                power = yr * yr + yi * yi
                best = power if best is None else jnp.maximum(best, power)
            if phase == 0 and u == 0:
                acc[block, row, :] = best
            else:
                acc[block, row, :] = jnp.maximum(acc[block, row, :], best)

        for index in range(cross_count):
            cross_piece(xa, 0, index)

        def phase_step(x_ref, y_new, phase, y_old, old_block, old_phase, x_next, next_block, key):
            share_p = -(-peak_count // RADIX)
            share_c = -(-(cross_count // 2) // RADIX)
            for k2 in range(RADIX):
                y_new[k2] = lax.dot_general(
                    x_ref[:, k2 * 2 * per_class : (k2 + 1) * 2 * per_class],
                    table[phase, k2],
                    (((1,), (0,)), ((), ())),
                    preferred_element_type=jnp.float32,
                )
                for index in range(k2 * share_p, min((k2 + 1) * share_p, peak_count)):
                    peak_piece(y_old, old_block, old_phase, index, key)
                for index in range(k2 * share_c, min((k2 + 1) * share_c, cross_count // 2)):
                    cross_piece(x_next, next_block, phase * (cross_count // 2) + index)

        def pair(p, carry):
            signs.clear()
            b = 2 * p
            last = jnp.where(p == 0, blocks, b - 1)
            after = jnp.where(b + 2 < blocks, b + 2, 0)
            phase_step(xa, ya, 0, yb, last, 1, xb, b + 1, 0)
            phase_step(xa, yb, 1, ya, b, 0, xb, b + 1, 1)
            phase_step(xb, ya, 0, yb, b, 1, xa, after, 2)
            phase_step(xb, yb, 1, ya, b + 1, 0, xa, after, 3)
            return carry

        load.wait()
        fetch.wait()
        lax.fori_loop(0, blocks // 2, pair, 0)
        signs.clear()
        for index in range(peak_count):
            peak_piece(yb, blocks - 1, 1, index, 0)

        square = wide[0] * wide[0] + wide[1] * wide[1]
        norm = jnp.sum(square, axis=1, keepdims=True)
        column = lax.broadcasted_iota(jnp.int32, (tpl_pad, segs), 1)
        result = jnp.zeros((tpl_pad, segs), jnp.float32)
        for s in range(segs):
            b, i = s // block_segs, s % block_segs
            top = jnp.max(acc[b, i * tpl_pad : (i + 1) * tpl_pad, :], axis=1, keepdims=True)
            result = jnp.where(column == s, top, result)
        out_ref[...] = (result / norm).T

    any_vmem = pl.BlockSpec(memory_space=pltpu.VMEM)
    peaks = pl.pallas_call(
        kernel,
        out_shape=jax.ShapeDtypeStruct((segs, tpl_pad), jnp.float32),
        in_specs=[pl.BlockSpec(memory_space=pltpu.HBM)]
        + [any_vmem] * 2
        + [pl.BlockSpec(memory_space=pltpu.HBM)],
        out_specs=any_vmem,
        scratch_shapes=[
            pltpu.SMEM((segs,), jnp.int32),
            pltpu.SemaphoreType.DMA,
            pltpu.VMEM((2, RADIX, 2 * per_class, span), jnp.bfloat16),
            pltpu.SemaphoreType.DMA,
            pltpu.VMEM((2, tpl_pad, bins), jnp.float32),
            pltpu.VMEM((segs, 2, bins), jnp.float32),
            pltpu.VMEM((2, segs, bins), jnp.float32),
            pltpu.VMEM((rows, 2 * bins), jnp.float32),
            pltpu.VMEM((rows, 2 * bins), jnp.float32),
            pltpu.VMEM((RADIX, rows, span), jnp.float32),
            pltpu.VMEM((RADIX, rows, span), jnp.float32),
            pltpu.VMEM((blocks + 1, rows, LANES), jnp.float32),
        ],
        compiler_params=pltpu.CompilerParams(vmem_limit_bytes=VMEM_MIB * 1024 * 1024),
        name="transform",
    )(valid_start, bank, strain, table)
    return peaks[:, :tpl_count]


def by_class(array):
    bins, two, columns = array.shape
    split = array.reshape(bins // RADIX, RADIX, two, columns)
    return split.transpose(3, 1, 2, 0).reshape(columns, two * bins)


def swap(block, axis, bit, dim):
    index = lax.axis_index(axis)
    count = lax.axis_size(axis)
    other = lax.ppermute(block, axis, [(j, j ^ (1 << bit)) for j in range(count)])
    low = jnp.concatenate([block, other], dim)
    high = jnp.concatenate([other, block], dim)
    return jnp.where((index >> bit) & 1 == 0, low, high)


def on_device(spectra, templates, valid_start):
    freq_count = lax.axis_size("freq")
    tpl_count = templates.shape[2] // freq_count
    exchange = lambda a: lax.all_to_all(a, "freq", 0, 0, tiled=True)
    to_all = lambda a: jnp.broadcast_to(a[None], (freq_count,) + a.shape)
    bits = freq_count.bit_length() - 1
    order = [bits - 1] + list(range(bits - 1))
    strain = swap(by_class(spectra)[None], "freq", order[0], 0)
    bank = lax.optimization_barrier(by_class(templates))
    bank = exchange(bank.reshape(freq_count, tpl_count, -1))
    table = make_table(templates.shape[0] * freq_count)
    strain = swap(strain, "freq", order[1], 0)
    for bit in order[2:]:
        strain = swap(strain, "freq", bit, 0)
    for bit in range(lax.axis_size("group").bit_length() - 1):
        strain = swap(strain, "group", bit, 1)
    place = [sum(((f >> bit) & 1) << i for i, bit in enumerate(order)) for f in range(freq_count)]
    peaks = exchange(to_all(transform(bank, strain, place, table, valid_start)))
    return peaks.transpose(0, 2, 1).reshape(templates.shape[2], -1)


def solution(mesh):
    in_specs = (P("freq", None, "group"), P("freq", None, "group"), P())
    out_specs = P("group", None)
    return jax.shard_map(
        on_device, mesh=mesh, in_specs=in_specs, out_specs=out_specs, check_vma=False
    )
```

time: 72.6 us -> 75.1 us (1.034)
  blocking collectives: 33 us -> 10.3 us
  waiting for transfers between devices: 8.84 us -> 20.6 us
  starting transfers between devices: 3.61 us -> 13.5 us
  local copies, waits for them, and re-layouts: 3.42 us -> 8.25 us
  other arithmetic: 0.91 us -> 0.14 us
    all_to_all x1, blocking collectives: 26.8 us -> 10.3 us  [on_device(): exchange = lambda a: lax.all_to_all(a, 'freq', 0, 0, tiled=True)]
    ppermute x3 -> x5, waiting for transfers between devices: 8.84 us -> 20.6 us  [swap(): other = lax.ppermute(block, axis, [(j, j ^ 1 << bit) for j in range(count)])]
    all_to_all x0 -> x1, starting transfers between devices: none -> 7.28 us  [on_device(): exchange = lambda a: lax.all_to_all(a, 'freq', 0, 0, tiled=True)]
    all_gather x1 -> x0, blocking collectives: 6.26 us -> none  [on_device(): segments = lax.all_gather(by_class(spectra), 'group', axis=0, tiled=True)]
    unnamed x12 -> x7, local copies, waits for them, and re-layouts: 0.14 us -> 5.31 us
    ppermute x3 -> x5, starting transfers between devices: 3.61 us -> 6.19 us  [swap(): other = lax.ppermute(block, axis, [(j, j ^ 1 << bit) for j in range(count)])]
    another operation x2 -> x1, local copies, waits for them, and re-layouts: 1.74 us -> 0.09 us  [on_device(): strain = swap(by_class(spectra)[None], 'freq', order[0], 0)]
    optimization_barrier x0 -> x1, local copies, waits for them, and re-layouts: none -> 1.15 us  [on_device(): bank = lax.optimization_barrier(by_class(templates))]
  transfers between devices with their start and end apart: 3 -> 6, of which waited for: 3 -> 4; matrix products, arithmetic and copies ran while one was open for 0% -> 2% of each run, Pallas kernels for 0% -> 2%
where the time goes in v2:
time: 75.1 us; the launch traced here: 74.7 us
  Pallas kernels  21.8 us (29%)
  waiting for transfers between devices  20.6 us (27%)
  starting transfers between devices  13.5 us (18%)
  blocking collectives  10.3 us (14%)
  local copies, waits for them, and re-layouts  8.25 us (11%)
    ppermute x5, waiting for transfers between devices, swap(): other = lax.ppermute(block, axis, [(j, j ^ 1 << bit) for j in range(count)])  20.6 us
    pallas_call x1, Pallas kernels, transform(): pl.pallas_call(kernel, out_shape=jax.ShapeDtypeStruct((segs, tpl_pad), jn...  20.1 us
    all_to_all x1, blocking collectives, on_device(): exchange = lambda a: lax.all_to_all(a, 'freq', 0, 0, tiled=True)  10.3 us
    all_to_all x1, starting transfers between devices, on_device(): exchange = lambda a: lax.all_to_all(a, 'freq', 0, 0, tiled=True)  7.28 us
    ppermute x5, starting transfers between devices, swap(): other = lax.ppermute(block, axis, [(j, j ^ 1 << bit) for j in range(count)])  6.19 us
    unnamed x7, local copies, waits for them, and re-layouts  5.31 us
    pallas_call x1, Pallas kernels, make_table(): pl.pallas_call(kernel, out_shape=jax.ShapeDtypeStruct((2, RADIX, 2 * per_...  1.63 us
  transfers between devices with their start and end apart: 6, of which 4 were waited for; matrix products, arithmetic and copies ran while one was open for 2% of the time, Pallas kernels for 2%

profile of v2, /device:TPU:0, one launch (start us, length us, event | category | flops | bytes accessed | tf_op | source)
XLA Modules:
  0.0 74.7 jit_solution(4151478544205471785)
XLA Ops:
  0.0 0.0 copy-start.2
  0.0 1.2 %copy.23 = bf16[256,2,640]{2,0,1:T(8,128)(2,1)S(1)} copy(bf16[256,2,640]{2,1,0:T(2,128)(2,1)} %param.5) | data formatting | bytes 1310720 | tf_op args[1]
  1.2 0.1 copy.18
  1.3 1.1 %copy.19 = bf16[640,512]{1,0:T(8,128)(2,1)} copy(bf16[640,512]{0,1:T(8,128)(2,1)S(1)} %bitcast.13) | data formatting | bytes 1310720 | tf_op jit(solution)/shard_map/optimization_barrier | solution.py:293
  2.4 7.3 %all-to-all-start = ((bf16[8,80,512]{2,1,0:T(8,128)(2,1)}), bf16[8,80,512]{2,1,0:T(8,128)(2,1)S(1)}, u32[]{:S(2)}, u32[]{:S(2)}) async-start(bf16[8,80,512]{2,1,0:T(8,128)(2,1)} %bitcast.3), calls=%async_computation | async-start | bytes 1310720 | tf_op jit(solution)/shard_map/all_to_all | solution.py:288
  9.7 0.8 %reshape.19 = bf16[32,8,2,4]{1,0,3,2:T(8,128)(2,1)S(1)} reshape(bf16[256,2,4]{0,2,1:T(4,128)(2,1)} %param.4) | data formatting | bytes 8192 | tf_op jit(solution)/shard_map/reshape | solution.py:272
  10.5 0.1 copy.20
  10.6 0.1 broadcast_in_dim_reshape.3
  10.7 2.9 %collective-permute-start = (bf16[1,4,512]{2,1,0:T(4,128)(2,1)S(1)}, bf16[1,4,512]{2,1,0:T(4,128)(2,1)S(1)}, u32[]{:S(2)}, u32[]{:S(2)}) collective-permute-start(bf16[1,4,512]{2,1,0:T(4,128)(2,1)S(1)} %broadcast_in_dim_reshape.3), channel_id=1, source_target_pairs={{0,4},{1,5},{2,6},{3,7},{4,0},{5,1},{6,2},{7,3},{8,12},{9,13},{10,... | collective-permute-start | bytes 12296 | tf_op jit(solution)/shard_map/ppermute | solution.py:279
  13.6 13.6 %collective-permute-done = bf16[1,4,512]{2,1,0:T(4,128)(2,1)S(1)} collective-permute-done((bf16[1,4,512]{2,1,0:T(4,128)(2,1)S(1)}, bf16[1,4,512]{2,1,0:T(4,128)(2,1)S(1)}, u32[]{:S(2)}, u32[]{:S(2)}) %collective-permute-start) | collective-permute-done | bytes 4128 | tf_op jit(solution)/shard_map/ppermute | solution.py:279
  27.2 1.5 %collective-permute-start.1 = (bf16[2,4,512]{2,1,0:T(4,128)(2,1)S(1)}, bf16[2,4,512]{2,1,0:T(4,128)(2,1)S(1)}, u32[]{:S(2)}, u32[]{:S(2)}) collective-permute-start(bf16[2,4,512]{2,1,0:T(4,128)(2,1)S(1)} %maximum_select_fusion.4), channel_id=1, source_target_pairs={{0,1},{1,0},{2,3},{3,2},{4,5},{5,4},{6,7},{7,6},{8,9},{9,8},{10,11... | collective-permute-start | bytes 24584 | tf_op jit(solution)/shard_map/ppermute | solution.py:279
  28.7 2.2 %collective-permute-done.1 = bf16[2,4,512]{2,1,0:T(4,128)(2,1)S(1)} collective-permute-done((bf16[2,4,512]{2,1,0:T(4,128)(2,1)S(1)}, bf16[2,4,512]{2,1,0:T(4,128)(2,1)S(1)}, u32[]{:S(2)}, u32[]{:S(2)}) %collective-permute-start.1) | collective-permute-done | bytes 8224 | tf_op jit(solution)/shard_map/ppermute | solution.py:279
  30.9 0.1 collective-permute-start.2
  31.0 3.7 %collective-permute-done.2 = bf16[4,4,512]{2,1,0:T(4,128)(2,1)S(1)} collective-permute-done((bf16[4,4,512]{2,1,0:T(4,128)(2,1)S(1)}, bf16[4,4,512]{2,1,0:T(4,128)(2,1)S(1)}, u32[]{:S(2)}, u32[]{:S(2)}) %collective-permute-start.2) | collective-permute-done | bytes 16416 | tf_op jit(solution)/shard_map/ppermute | solution.py:279
  34.8 0.1 collective-permute-start.3
  34.8 1.2 %collective-permute-done.3 = bf16[8,4,512]{2,1,0:T(4,128)(2,1)S(1)} collective-permute-done((bf16[8,4,512]{2,1,0:T(4,128)(2,1)S(1)}, bf16[8,4,512]{2,1,0:T(4,128)(2,1)S(1)}, u32[]{:S(2)}, u32[]{:S(2)}) %collective-permute-start.3) | collective-permute-done | bytes 32800 | tf_op jit(solution)/shard_map/ppermute | solution.py:279
  36.0 0.1 maximum_select_fusion.1
  36.1 1.6 %collective-permute-start.4 = (bf16[8,8,512]{2,1,0:T(8,128)(2,1)S(1)}, bf16[8,8,512]{2,1,0:T(8,128)(2,1)S(1)}, u32[]{:S(2)}, u32[]{:S(2)}) collective-permute-start(bf16[8,8,512]{2,1,0:T(8,128)(2,1)S(1)} %maximum_select_fusion.1), channel_id=1, source_target_pairs={{0,16},{8,24},{16,0},{24,8},{1,17},{9,25},{17,1},{25,9},{2,18},{10... | collective-permute-start | bytes 196616 | tf_op jit(solution)/shard_map/ppermute | solution.py:279
  37.7 0.0 copy-start.1
  37.7 0.9 %copy-done.1 = f32[40,2,512]{2,1,0:T(2,128)S(1)} copy-done((f32[40,2,512]{2,1,0:T(2,128)S(1)}, f32[40,2,512]{2,1,0:T(2,128)}, u32[]{:S(2)}) %copy-start.1) | copy-done | bytes 163864
  38.6 1.6 %table.1.table_ref = bf16[2,8,512,512]{3,2,1,0:T(8,128)(2,1)S(1)} custom-call(f32[40,2,512]{2,1,0:T(2,128)S(1)} %copy-done.1), custom_call_target="tpu_custom_call" | custom-call | tf_op jit(solution)/shard_map/table/pallas_call | solution.py:61
  40.2 0.0 copy-start
  40.2 3.2 %copy-done = bf16[2,8,512,512]{3,2,1,0:T(8,128)(2,1)} copy-done((bf16[2,8,512,512]{3,2,1,0:T(8,128)(2,1)}, bf16[2,8,512,512]{3,2,1,0:T(8,128)(2,1)S(1)}, u32[]{:S(2)}) %copy-start) | copy-done | bytes 8388632
  43.5 0.0 collective-permute-done.4
  43.5 0.0 all-to-all-done.bank_ref
  43.5 0.0 copy-done.2
  43.5 20.1 %transform.1 = f32[16,80]{1,0:T(8,128)S(1)} custom-call(s32[16]{0:T(128)S(1)} %copy-done.2, bf16[8,80,512]{2,1,0:T(8,128)(2,1)S(1)} %all-to-all-done.bank_ref, bf16[8,16,512]{2,1,0:T(8,128)(2,1)S(1)} %maximum_select_fusion.strain_ref, bf16[2,8,512,512]{3,2,1,0:T(8,128)(2,1)} %copy-done), custom_call_target="tpu_custom_call" | custom-call | tf_op jit(solution)/shard_map/transform/pallas_call | solution.py:243
  63.7 10.3 %all_to_all.10 = f32[8,16,80]{2,1,0:T(8,128)S(1)} all-to-all(f32[8,16,80]{2,1,0:T(8,128)S(1)} %broadcast_in_dim.2), channel_id=1, replica_groups=mesh['group'=4,'freq'=8] {'freq'}, dimensions={0} | all-to-all | bytes 81920 | tf_op jit(solution)/shard_map/all_to_all | solution.py:288
  74.0 0.7 reshape.20
  (6 shorter events, 0.1 us)
Async XLA Ops:
  0.0 43.5 %copy-start.2 = (s32[16]{0:T(128)S(1)}, s32[16]{0:T(128)}, u32[]{:S(2)}) copy-start(s32[16]{0:T(128)} %start_hbm.1) | copy-start | bytes 196
  2.4 41.1 %all-to-all-start = ((bf16[8,80,512]{2,1,0:T(8,128)(2,1)}), bf16[8,80,512]{2,1,0:T(8,128)(2,1)S(1)}, u32[]{:S(2)}, u32[]{:S(2)}) async-start(bf16[8,80,512]{2,1,0:T(8,128)(2,1)} %bitcast.3), calls=%async_computation | async-start | bytes 1310720 | tf_op jit(solution)/shard_map/all_to_all | solution.py:288
  10.7 16.5 %collective-permute-start = (bf16[1,4,512]{2,1,0:T(4,128)(2,1)S(1)}, bf16[1,4,512]{2,1,0:T(4,128)(2,1)S(1)}, u32[]{:S(2)}, u32[]{:S(2)}) collective-permute-start(bf16[1,4,512]{2,1,0:T(4,128)(2,1)S(1)} %broadcast_in_dim_reshape.3), channel_id=1, source_target_pairs={{0,4},{1,5},{2,6},{3,7},{4,0},{5,1},{6,2},{7,3},{8,12},{9,13},{10,... | collective-permute-start | bytes 12296 | tf_op jit(solution)/shard_map/ppermute | solution.py:279
  27.2 3.7 %collective-permute-start.1 = (bf16[2,4,512]{2,1,0:T(4,128)(2,1)S(1)}, bf16[2,4,512]{2,1,0:T(4,128)(2,1)S(1)}, u32[]{:S(2)}, u32[]{:S(2)}) collective-permute-start(bf16[2,4,512]{2,1,0:T(4,128)(2,1)S(1)} %maximum_select_fusion.4), channel_id=1, source_target_pairs={{0,1},{1,0},{2,3},{3,2},{4,5},{5,4},{6,7},{7,6},{8,9},{9,8},{10,11... | collective-permute-start | bytes 24584 | tf_op jit(solution)/shard_map/ppermute | solution.py:279
  30.9 3.8 %collective-permute-start.2 = (bf16[4,4,512]{2,1,0:T(4,128)(2,1)S(1)}, bf16[4,4,512]{2,1,0:T(4,128)(2,1)S(1)}, u32[]{:S(2)}, u32[]{:S(2)}) collective-permute-start(bf16[4,4,512]{2,1,0:T(4,128)(2,1)S(1)} %maximum_select_fusion.3), channel_id=1, source_target_pairs={{0,2},{1,3},{2,0},{3,1},{4,6},{5,7},{6,4},{7,5},{8,10},{9,11},{10,... | collective-permute-start | bytes 49160 | tf_op jit(solution)/shard_map/ppermute | solution.py:279
  34.8 1.3 %collective-permute-start.3 = (bf16[8,4,512]{2,1,0:T(4,128)(2,1)S(1)}, bf16[8,4,512]{2,1,0:T(4,128)(2,1)S(1)}, u32[]{:S(2)}, u32[]{:S(2)}) collective-permute-start(bf16[8,4,512]{2,1,0:T(4,128)(2,1)S(1)} %maximum_select_fusion.2), channel_id=1, source_target_pairs={{0,8},{8,0},{16,24},{24,16},{1,9},{9,1},{17,25},{25,17},{2,10},{10... | collective-permute-start | bytes 98312 | tf_op jit(solution)/shard_map/ppermute | solution.py:279
  36.1 7.4 %collective-permute-start.4 = (bf16[8,8,512]{2,1,0:T(8,128)(2,1)S(1)}, bf16[8,8,512]{2,1,0:T(8,128)(2,1)S(1)}, u32[]{:S(2)}, u32[]{:S(2)}) collective-permute-start(bf16[8,8,512]{2,1,0:T(8,128)(2,1)S(1)} %maximum_select_fusion.1), channel_id=1, source_target_pairs={{0,16},{8,24},{16,0},{24,8},{1,17},{9,25},{17,1},{25,9},{2,18},{10... | collective-permute-start | bytes 196616 | tf_op jit(solution)/shard_map/ppermute | solution.py:279
  37.7 0.9 %copy-start.1 = (f32[40,2,512]{2,1,0:T(2,128)S(1)}, f32[40,2,512]{2,1,0:T(2,128)}, u32[]{:S(2)}) copy-start(f32[40,2,512]{2,1,0:T(2,128)} %constant.16.clone.factor_ref) | copy-start | bytes 491524
  40.2 3.2 %copy-start = (bf16[2,8,512,512]{3,2,1,0:T(8,128)(2,1)}, bf16[2,8,512,512]{3,2,1,0:T(8,128)(2,1)S(1)}, u32[]{:S(2)}) copy-start(bf16[2,8,512,512]{3,2,1,0:T(8,128)(2,1)S(1)} %table.1.table_ref) | copy-start | bytes 25165828

commit v3 on v2

--- a/solution.py
+++ b/solution.py
@@ -1,3 +1,4 @@
+import functools
 import math
 
 import jax
@@ -30,6 +31,7 @@
     per_class = bins // RADIX
     span = N // RADIX
     half = span // 2
+    tiles = half // LANES
 
     def kernel(factor_ref, table, fine):
         for row in range(16):
@@ -48,11 +50,12 @@
                 c = (ar * lr - ai * li).astype(jnp.bfloat16)
                 s = (ar * li + ai * lr).astype(jnp.bfloat16)
                 for ph in range(2):
-                    t = slice(ph * half, (ph + 1) * half)
-                    table[ph, k2, pl.ds(at, 16), :half] = c[:, t]
-                    table[ph, k2, pl.ds(at, 16), half:] = s[:, t]
-                    table[ph, k2, pl.ds(per_class + at, 16), :half] = -s[:, t]
-                    table[ph, k2, pl.ds(per_class + at, 16), half:] = c[:, t]
+                    for u in range(tiles):
+                        t = slice(ph * half + u * LANES, ph * half + (u + 1) * LANES)
+                        table[ph, k2, u, pl.ds(at, 16), :] = c[:, t]
+                        table[ph, k2, tiles + u, pl.ds(at, 16), :] = s[:, t]
+                        table[ph, k2, u, pl.ds(per_class + at, 16), :] = -s[:, t]
+                        table[ph, k2, tiles + u, pl.ds(per_class + at, 16), :] = c[:, t]
             return carry
 
         lax.fori_loop(0, per_class // 16, table_rows, 0)
@@ -60,7 +63,7 @@
     any_vmem = pl.BlockSpec(memory_space=pltpu.VMEM)
     return pl.pallas_call(
         kernel,
-        out_shape=jax.ShapeDtypeStruct((2, RADIX, 2 * per_class, span), jnp.bfloat16),
+        out_shape=jax.ShapeDtypeStruct((2, RADIX, 2 * tiles, 2 * per_class, LANES), jnp.bfloat16),
         in_specs=[any_vmem],
         out_specs=any_vmem,
         scratch_shapes=[pltpu.VMEM((2, 16, span), jnp.float32)],
@@ -86,9 +89,21 @@
         bank = jnp.pad(bank, ((0, 0), (0, tpl_pad - tpl_count), (0, 0)))
     root = np.float32(math.sqrt(0.5))
 
-    def kernel(start_hbm, bank_ref, strain_ref, table_ref, out_ref, start_ref, start_sem, table, sem, wide, lines, flat, xa, xb, ya, yb, acc):
-        load = pltpu.make_async_copy(table_ref, table, sem)
-        load.start()
+    def kernel(*refs):
+        pl.run_scoped(
+            functools.partial(body, *refs),
+            pltpu.VMEM((2, RADIX, 2 * half // LANES, 2 * per_class, LANES), jnp.bfloat16),
+            pltpu.VMEM((rows, 2 * bins), jnp.bfloat16),
+            pltpu.VMEM((rows, 2 * bins), jnp.bfloat16),
+        )
+
+    def body(
+        start_hbm, bank_ref, strain_ref, table_ref, out_ref, start_ref, start_sem, sem, wide, lines, flat, ya, yb, acc,
+        table, xa, xb,
+    ):
+        loads = [pltpu.make_async_copy(table_ref.at[ph], table.at[ph], sem.at[ph]) for ph in range(2)]
+        for load in loads:
+            load.start()
         fetch = pltpu.make_async_copy(start_hbm, start_ref, start_sem)
         fetch.start()
 
@@ -131,13 +146,16 @@
                 [jnp.broadcast_to(lines[block * block_segs + i, c : c + 1, at], (8, LANES)) for c in range(2)]
                 for i in range(block_segs)
             ]
-            for t in range(0, tpl_pad, 8):
-                h0 = wide[0, t : t + 8, at]
-                h1 = wide[1, t : t + 8, at]
+            shape = (2, 8, LANES)
+            for t in range(0, tpl_pad, 16):
+                h0 = wide[0, t : t + 16, at].reshape(shape)
+                h1 = wide[1, t : t + 16, at].reshape(shape)
                 for i in range(block_segs):
-                    row = slice(i * tpl_pad + t, i * tpl_pad + t + 8)
-                    x_ref[row, col : col + LANES] = h0 * d[i][0] + h1 * d[i][1]
-                    x_ref[row, col_im : col_im + LANES] = h0 * d[i][1] - h1 * d[i][0]
+                    row = slice(i * tpl_pad + t, i * tpl_pad + t + 16)
+                    re = (h0 * d[i][0] + h1 * d[i][1]).reshape(16, LANES)
+                    im = (h0 * d[i][1] - h1 * d[i][0]).reshape(16, LANES)
+                    x_ref[row, col : col + LANES] = re.astype(jnp.bfloat16)
+                    x_ref[row, col_im : col_im + LANES] = im.astype(jnp.bfloat16)
 
         cross_count = RADIX * tiles
         lane8 = lax.broadcasted_iota(jnp.int32, (8, LANES), 1)
@@ -196,40 +214,35 @@
         for index in range(cross_count):
             cross_piece(xa, 0, index)
 
-        def phase_step(x_ref, y_new, phase, y_old, old_block, old_phase, x_next, next_block, key):
-            share_p = -(-peak_count // RADIX)
-            share_c = -(-(cross_count // 2) // RADIX)
+        share_p = -(-peak_count // RADIX)
+        share_c = -(-(cross_count // 2) // RADIX)
+        x_refs, y_refs = (xa, xb), (ya, yb)
+        fetch.wait()
+        for step in range(2 * blocks):
+            block, phase = divmod(step, 2)
+            if block == 0:
+                loads[phase].wait()
+            signs.clear()
             for k2 in range(RADIX):
-                y_new[k2] = lax.dot_general(
-                    x_ref[:, k2 * 2 * per_class : (k2 + 1) * 2 * per_class],
-                    table[phase, k2],
+                tile = [table[phase, k2, n] for n in range(2 * lane_tiles)]
+                y_refs[phase][k2, :rows, :span] = lax.dot_general(
+                    x_refs[block % 2][:, k2 * 2 * per_class : (k2 + 1) * 2 * per_class],
+                    jnp.concatenate(tile, 1),
                     (((1,), (0,)), ((), ())),
                     preferred_element_type=jnp.float32,
                 )
-                for index in range(k2 * share_p, min((k2 + 1) * share_p, peak_count)):
-                    peak_piece(y_old, old_block, old_phase, index, key)
-                for index in range(k2 * share_c, min((k2 + 1) * share_c, cross_count // 2)):
-                    cross_piece(x_next, next_block, phase * (cross_count // 2) + index)
-
-        def pair(p, carry):
-            signs.clear()
-            b = 2 * p
-            last = jnp.where(p == 0, blocks, b - 1)
-            after = jnp.where(b + 2 < blocks, b + 2, 0)
-            phase_step(xa, ya, 0, yb, last, 1, xb, b + 1, 0)
-            phase_step(xa, yb, 1, ya, b, 0, xb, b + 1, 1)
-            phase_step(xb, ya, 0, yb, b, 1, xa, after, 2)
-            phase_step(xb, yb, 1, ya, b + 1, 0, xa, after, 3)
-            return carry
-
-        load.wait()
-        fetch.wait()
-        lax.fori_loop(0, blocks // 2, pair, 0)
+                if step > 0:
+                    before, before_phase = divmod(step - 1, 2)
+                    for index in range(k2 * share_p, min((k2 + 1) * share_p, peak_count)):
+                        peak_piece(y_refs[before_phase], before, before_phase, index, step)
+                if block + 1 < blocks:
+                    for index in range(k2 * share_c, min((k2 + 1) * share_c, cross_count // 2)):
+                        cross_piece(x_refs[(block + 1) % 2], block + 1, phase * (cross_count // 2) + index)
         signs.clear()
         for index in range(peak_count):
             peak_piece(yb, blocks - 1, 1, index, 0)
 
-        square = wide[0] * wide[0] + wide[1] * wide[1]
+        square = wide[0, :, :bins] * wide[0, :, :bins] + wide[1, :, :bins] * wide[1, :, :bins]
         norm = jnp.sum(square, axis=1, keepdims=True)
         column = lax.broadcasted_iota(jnp.int32, (tpl_pad, segs), 1)
         result = jnp.zeros((tpl_pad, segs), jnp.float32)
@@ -250,16 +263,13 @@
         scratch_shapes=[
             pltpu.SMEM((segs,), jnp.int32),
             pltpu.SemaphoreType.DMA,
-            pltpu.VMEM((2, RADIX, 2 * per_class, span), jnp.bfloat16),
-            pltpu.SemaphoreType.DMA,
-            pltpu.VMEM((2, tpl_pad, bins), jnp.float32),
+            pltpu.SemaphoreType.DMA((2,)),
+            pltpu.VMEM((2, tpl_pad, bins + LANES), jnp.float32),
             pltpu.VMEM((segs, 2, bins), jnp.float32),
             pltpu.VMEM((2, segs, bins), jnp.float32),
-            pltpu.VMEM((rows, 2 * bins), jnp.float32),
-            pltpu.VMEM((rows, 2 * bins), jnp.float32),
-            pltpu.VMEM((RADIX, rows, span), jnp.float32),
-            pltpu.VMEM((RADIX, rows, span), jnp.float32),
-            pltpu.VMEM((blocks + 1, rows, LANES), jnp.float32),
+            pltpu.VMEM((RADIX, rows + 8, span + LANES), jnp.float32),
+            pltpu.VMEM((RADIX, rows + 8, span + LANES), jnp.float32),
+            pltpu.VMEM((blocks, rows, LANES), jnp.float32),
         ],
         compiler_params=pltpu.CompilerParams(vmem_limit_bytes=VMEM_MIB * 1024 * 1024),
         name="transform",

time: 75.1 us -> 74.6 us (level)
    pallas_call x1, Pallas kernels: 20.1 us -> 19.3 us  [transform(): pl.pallas_call(kernel, out_shape=jax.ShapeDtypeStruct((segs, tpl_pad), jn...]
  transfers between devices with their start and end apart: 6 -> 6, of which waited for: 4 -> 4; matrix products, arithmetic and copies ran while one was open for 2% -> 2% of each run, Pallas kernels for 2% -> 3%
where the time goes in v3:
time: 74.6 us; the launch traced here: 74.3 us
  Pallas kernels  21.3 us (29%)
  waiting for transfers between devices  20.6 us (28%)
  starting transfers between devices  13.5 us (18%)
  blocking collectives  10.3 us (14%)
  local copies, waits for them, and re-layouts  8.26 us (11%)
    ppermute x5, waiting for transfers between devices, swap(): other = lax.ppermute(block, axis, [(j, j ^ 1 << bit) for j in range(count)])  20.6 us
    pallas_call x1, Pallas kernels, transform(): pl.pallas_call(kernel, out_shape=jax.ShapeDtypeStruct((segs, tpl_pad), jn...  19.3 us
    all_to_all x1, blocking collectives, on_device(): exchange = lambda a: lax.all_to_all(a, 'freq', 0, 0, tiled=True)  10.3 us
    all_to_all x1, starting transfers between devices, on_device(): exchange = lambda a: lax.all_to_all(a, 'freq', 0, 0, tiled=True)  7.28 us
    ppermute x5, starting transfers between devices, swap(): other = lax.ppermute(block, axis, [(j, j ^ 1 << bit) for j in range(count)])  6.19 us
    unnamed x7, local copies, waits for them, and re-layouts  5.31 us
    pallas_call x1, Pallas kernels, make_table(): pl.pallas_call(kernel, out_shape=jax.ShapeDtypeStruct((2, RADIX, 2 * tile...  1.96 us
  transfers between devices with their start and end apart: 6, of which 4 were waited for; matrix products, arithmetic and copies ran while one was open for 2% of the time, Pallas kernels for 3%

profile of v3, /device:TPU:0, one launch (start us, length us, event | category | flops | bytes accessed | tf_op | source)
XLA Modules:
  0.0 74.3 jit_solution(7346933120214539300)
XLA Ops:
  0.0 0.0 copy-start.2
  0.0 1.2 %copy.23 = bf16[256,2,640]{2,0,1:T(8,128)(2,1)S(1)} copy(bf16[256,2,640]{2,1,0:T(2,128)(2,1)} %param.5) | data formatting | bytes 1310720 | tf_op args[1]
  1.2 0.1 copy.18
  1.3 1.1 %copy.19 = bf16[640,512]{1,0:T(8,128)(2,1)} copy(bf16[640,512]{0,1:T(8,128)(2,1)S(1)} %bitcast.13) | data formatting | bytes 1310720 | tf_op jit(solution)/shard_map/optimization_barrier | solution.py:303
  2.4 7.3 %all-to-all-start = ((bf16[8,80,512]{2,1,0:T(8,128)(2,1)}), bf16[8,80,512]{2,1,0:T(8,128)(2,1)S(1)}, u32[]{:S(2)}, u32[]{:S(2)}) async-start(bf16[8,80,512]{2,1,0:T(8,128)(2,1)} %bitcast.3), calls=%async_computation | async-start | bytes 1310720 | tf_op jit(solution)/shard_map/all_to_all | solution.py:298
  9.7 0.8 %reshape.19 = bf16[32,8,2,4]{1,0,3,2:T(8,128)(2,1)S(1)} reshape(bf16[256,2,4]{0,2,1:T(4,128)(2,1)} %param.4) | data formatting | bytes 8192 | tf_op jit(solution)/shard_map/reshape | solution.py:282
  10.5 0.1 copy.20
  10.6 0.1 broadcast_in_dim_reshape.3
  10.7 2.9 %collective-permute-start = (bf16[1,4,512]{2,1,0:T(4,128)(2,1)S(1)}, bf16[1,4,512]{2,1,0:T(4,128)(2,1)S(1)}, u32[]{:S(2)}, u32[]{:S(2)}) collective-permute-start(bf16[1,4,512]{2,1,0:T(4,128)(2,1)S(1)} %broadcast_in_dim_reshape.3), channel_id=1, source_target_pairs={{0,4},{1,5},{2,6},{3,7},{4,0},{5,1},{6,2},{7,3},{8,12},{9,13},{10,... | collective-permute-start | bytes 12296 | tf_op jit(solution)/shard_map/ppermute | solution.py:289
  13.6 13.6 %collective-permute-done = bf16[1,4,512]{2,1,0:T(4,128)(2,1)S(1)} collective-permute-done((bf16[1,4,512]{2,1,0:T(4,128)(2,1)S(1)}, bf16[1,4,512]{2,1,0:T(4,128)(2,1)S(1)}, u32[]{:S(2)}, u32[]{:S(2)}) %collective-permute-start) | collective-permute-done | bytes 4128 | tf_op jit(solution)/shard_map/ppermute | solution.py:289
  27.2 1.5 %collective-permute-start.1 = (bf16[2,4,512]{2,1,0:T(4,128)(2,1)S(1)}, bf16[2,4,512]{2,1,0:T(4,128)(2,1)S(1)}, u32[]{:S(2)}, u32[]{:S(2)}) collective-permute-start(bf16[2,4,512]{2,1,0:T(4,128)(2,1)S(1)} %maximum_select_fusion.4), channel_id=1, source_target_pairs={{0,1},{1,0},{2,3},{3,2},{4,5},{5,4},{6,7},{7,6},{8,9},{9,8},{10,11... | collective-permute-start | bytes 24584 | tf_op jit(solution)/shard_map/ppermute | solution.py:289
  28.7 2.2 %collective-permute-done.1 = bf16[2,4,512]{2,1,0:T(4,128)(2,1)S(1)} collective-permute-done((bf16[2,4,512]{2,1,0:T(4,128)(2,1)S(1)}, bf16[2,4,512]{2,1,0:T(4,128)(2,1)S(1)}, u32[]{:S(2)}, u32[]{:S(2)}) %collective-permute-start.1) | collective-permute-done | bytes 8224 | tf_op jit(solution)/shard_map/ppermute | solution.py:289
  30.9 0.1 collective-permute-start.2
  31.0 3.7 %collective-permute-done.2 = bf16[4,4,512]{2,1,0:T(4,128)(2,1)S(1)} collective-permute-done((bf16[4,4,512]{2,1,0:T(4,128)(2,1)S(1)}, bf16[4,4,512]{2,1,0:T(4,128)(2,1)S(1)}, u32[]{:S(2)}, u32[]{:S(2)}) %collective-permute-start.2) | collective-permute-done | bytes 16416 | tf_op jit(solution)/shard_map/ppermute | solution.py:289
  34.8 0.1 collective-permute-start.3
  34.8 1.2 %collective-permute-done.3 = bf16[8,4,512]{2,1,0:T(4,128)(2,1)S(1)} collective-permute-done((bf16[8,4,512]{2,1,0:T(4,128)(2,1)S(1)}, bf16[8,4,512]{2,1,0:T(4,128)(2,1)S(1)}, u32[]{:S(2)}, u32[]{:S(2)}) %collective-permute-start.3) | collective-permute-done | bytes 32800 | tf_op jit(solution)/shard_map/ppermute | solution.py:289
  36.0 0.1 maximum_select_fusion.1
  36.1 1.6 %collective-permute-start.4 = (bf16[8,8,512]{2,1,0:T(8,128)(2,1)S(1)}, bf16[8,8,512]{2,1,0:T(8,128)(2,1)S(1)}, u32[]{:S(2)}, u32[]{:S(2)}) collective-permute-start(bf16[8,8,512]{2,1,0:T(8,128)(2,1)S(1)} %maximum_select_fusion.1), channel_id=1, source_target_pairs={{0,16},{8,24},{16,0},{24,8},{1,17},{9,25},{17,1},{25,9},{2,18},{10... | collective-permute-start | bytes 196616 | tf_op jit(solution)/shard_map/ppermute | solution.py:289
  37.7 0.0 copy-start.1
  37.7 0.9 %copy-done.1 = f32[40,2,512]{2,1,0:T(2,128)S(1)} copy-done((f32[40,2,512]{2,1,0:T(2,128)S(1)}, f32[40,2,512]{2,1,0:T(2,128)}, u32[]{:S(2)}) %copy-start.1) | copy-done | bytes 163864
  38.6 2.0 %table.1.refs_3_ = bf16[2,8,4,512,128]{4,3,2,1,0:T(8,128)(2,1)S(1)} custom-call(f32[40,2,512]{2,1,0:T(2,128)S(1)} %copy-done.1), custom_call_target="tpu_custom_call" | custom-call | tf_op jit(solution)/shard_map/table/pallas_call | solution.py:64
  40.6 0.0 copy-start
  40.6 3.2 %copy-done = bf16[2,8,4,512,128]{4,3,2,1,0:T(8,128)(2,1)} copy-done((bf16[2,8,4,512,128]{4,3,2,1,0:T(8,128)(2,1)}, bf16[2,8,4,512,128]{4,3,2,1,0:T(8,128)(2,1)S(1)}, u32[]{:S(2)}) %copy-start) | copy-done | bytes 8388632
  43.8 0.0 collective-permute-done.4
  43.8 0.0 all-to-all-done.refs_1_
  43.8 0.0 copy-done.2
  43.9 19.3 %transform.1 = f32[16,80]{1,0:T(8,128)S(1)} custom-call(s32[16]{0:T(128)S(1)} %copy-done.2, bf16[8,80,512]{2,1,0:T(8,128)(2,1)S(1)} %all-to-all-done.refs_1_, bf16[8,16,512]{2,1,0:T(8,128)(2,1)S(1)} %maximum_select_fusion.refs_2_, bf16[2,8,4,512,128]{4,3,2,1,0:T(8,128)(2,1)} %copy-done), custom_call_target="tpu_custom_call" | custom-call | tf_op jit(solution)/shard_map/transform/pallas_call | solution.py:256
  63.2 10.3 %all_to_all.10 = f32[8,16,80]{2,1,0:T(8,128)S(1)} all-to-all(f32[8,16,80]{2,1,0:T(8,128)S(1)} %broadcast_in_dim.2), channel_id=1, replica_groups=mesh['group'=4,'freq'=8] {'freq'}, dimensions={0} | all-to-all | bytes 81920 | tf_op jit(solution)/shard_map/all_to_all | solution.py:298
  73.6 0.7 reshape.20
  (6 shorter events, 0.1 us)
Async XLA Ops:
  0.0 43.8 %copy-start.2 = (s32[16]{0:T(128)S(1)}, s32[16]{0:T(128)}, u32[]{:S(2)}) copy-start(s32[16]{0:T(128)} %refs_0_.1) | copy-start | bytes 196
  2.4 41.4 %all-to-all-start = ((bf16[8,80,512]{2,1,0:T(8,128)(2,1)}), bf16[8,80,512]{2,1,0:T(8,128)(2,1)S(1)}, u32[]{:S(2)}, u32[]{:S(2)}) async-start(bf16[8,80,512]{2,1,0:T(8,128)(2,1)} %bitcast.3), calls=%async_computation | async-start | bytes 1310720 | tf_op jit(solution)/shard_map/all_to_all | solution.py:298
  10.7 16.5 %collective-permute-start = (bf16[1,4,512]{2,1,0:T(4,128)(2,1)S(1)}, bf16[1,4,512]{2,1,0:T(4,128)(2,1)S(1)}, u32[]{:S(2)}, u32[]{:S(2)}) collective-permute-start(bf16[1,4,512]{2,1,0:T(4,128)(2,1)S(1)} %broadcast_in_dim_reshape.3), channel_id=1, source_target_pairs={{0,4},{1,5},{2,6},{3,7},{4,0},{5,1},{6,2},{7,3},{8,12},{9,13},{10,... | collective-permute-start | bytes 12296 | tf_op jit(solution)/shard_map/ppermute | solution.py:289
  27.2 3.7 %collective-permute-start.1 = (bf16[2,4,512]{2,1,0:T(4,128)(2,1)S(1)}, bf16[2,4,512]{2,1,0:T(4,128)(2,1)S(1)}, u32[]{:S(2)}, u32[]{:S(2)}) collective-permute-start(bf16[2,4,512]{2,1,0:T(4,128)(2,1)S(1)} %maximum_select_fusion.4), channel_id=1, source_target_pairs={{0,1},{1,0},{2,3},{3,2},{4,5},{5,4},{6,7},{7,6},{8,9},{9,8},{10,11... | collective-permute-start | bytes 24584 | tf_op jit(solution)/shard_map/ppermute | solution.py:289
  30.9 3.8 %collective-permute-start.2 = (bf16[4,4,512]{2,1,0:T(4,128)(2,1)S(1)}, bf16[4,4,512]{2,1,0:T(4,128)(2,1)S(1)}, u32[]{:S(2)}, u32[]{:S(2)}) collective-permute-start(bf16[4,4,512]{2,1,0:T(4,128)(2,1)S(1)} %maximum_select_fusion.3), channel_id=1, source_target_pairs={{0,2},{1,3},{2,0},{3,1},{4,6},{5,7},{6,4},{7,5},{8,10},{9,11},{10,... | collective-permute-start | bytes 49160 | tf_op jit(solution)/shard_map/ppermute | solution.py:289
  34.8 1.3 %collective-permute-start.3 = (bf16[8,4,512]{2,1,0:T(4,128)(2,1)S(1)}, bf16[8,4,512]{2,1,0:T(4,128)(2,1)S(1)}, u32[]{:S(2)}, u32[]{:S(2)}) collective-permute-start(bf16[8,4,512]{2,1,0:T(4,128)(2,1)S(1)} %maximum_select_fusion.2), channel_id=1, source_target_pairs={{0,8},{8,0},{16,24},{24,16},{1,9},{9,1},{17,25},{25,17},{2,10},{10... | collective-permute-start | bytes 98312 | tf_op jit(solution)/shard_map/ppermute | solution.py:289
  36.1 7.7 %collective-permute-start.4 = (bf16[8,8,512]{2,1,0:T(8,128)(2,1)S(1)}, bf16[8,8,512]{2,1,0:T(8,128)(2,1)S(1)}, u32[]{:S(2)}, u32[]{:S(2)}) collective-permute-start(bf16[8,8,512]{2,1,0:T(8,128)(2,1)S(1)} %maximum_select_fusion.1), channel_id=1, source_target_pairs={{0,16},{8,24},{16,0},{24,8},{1,17},{9,25},{17,1},{25,9},{2,18},{10... | collective-permute-start | bytes 196616 | tf_op jit(solution)/shard_map/ppermute | solution.py:289
  37.7 0.9 %copy-start.1 = (f32[40,2,512]{2,1,0:T(2,128)S(1)}, f32[40,2,512]{2,1,0:T(2,128)}, u32[]{:S(2)}) copy-start(f32[40,2,512]{2,1,0:T(2,128)} %constant.16.clone.factor_ref) | copy-start | bytes 491524
  40.6 3.2 %copy-start = (bf16[2,8,4,512,128]{4,3,2,1,0:T(8,128)(2,1)}, bf16[2,8,4,512,128]{4,3,2,1,0:T(8,128)(2,1)S(1)}, u32[]{:S(2)}) copy-start(bf16[2,8,4,512,128]{4,3,2,1,0:T(8,128)(2,1)S(1)} %table.1.refs_3_) | copy-start | bytes 25165828

commit v4 on v3

--- a/solution.py
+++ b/solution.py
@@ -102,8 +102,7 @@
         table, xa, xb,
     ):
         loads = [pltpu.make_async_copy(table_ref.at[ph], table.at[ph], sem.at[ph]) for ph in range(2)]
-        for load in loads:
-            load.start()
+        loads[0].start()
         fetch = pltpu.make_async_copy(start_hbm, start_ref, start_sem)
         fetch.start()
 
@@ -222,6 +221,8 @@
             block, phase = divmod(step, 2)
             if block == 0:
                 loads[phase].wait()
+                if phase == 0:
+                    loads[1].start()
             signs.clear()
             for k2 in range(RADIX):
                 tile = [table[phase, k2, n] for n in range(2 * lane_tiles)]

time: 74.6 us -> 75.2 us (level)
  no operation moved by 1% of the time
where the time goes in v4:
time: 75.2 us; the launch traced here: 74.8 us
  Pallas kernels  21.8 us (29%)
  waiting for transfers between devices  20.6 us (27%)
  starting transfers between devices  13.5 us (18%)
  blocking collectives  10.3 us (14%)
  local copies, waits for them, and re-layouts  8.26 us (11%)
    ppermute x5, waiting for transfers between devices, swap(): other = lax.ppermute(block, axis, [(j, j ^ 1 << bit) for j in range(count)])  20.6 us
    pallas_call x1, Pallas kernels, transform(): pl.pallas_call(kernel, out_shape=jax.ShapeDtypeStruct((segs, tpl_pad), jn...  19.9 us
    all_to_all x1, blocking collectives, on_device(): exchange = lambda a: lax.all_to_all(a, 'freq', 0, 0, tiled=True)  10.3 us
    all_to_all x1, starting transfers between devices, on_device(): exchange = lambda a: lax.all_to_all(a, 'freq', 0, 0, tiled=True)  7.28 us
    ppermute x5, starting transfers between devices, swap(): other = lax.ppermute(block, axis, [(j, j ^ 1 << bit) for j in range(count)])  6.19 us
    unnamed x7, local copies, waits for them, and re-layouts  5.31 us
    pallas_call x1, Pallas kernels, make_table(): pl.pallas_call(kernel, out_shape=jax.ShapeDtypeStruct((2, RADIX, 2 * tile...  1.96 us
  transfers between devices with their start and end apart: 6, of which 4 were waited for; matrix products, arithmetic and copies ran while one was open for 2% of the time, Pallas kernels for 3%

profile of v4, /device:TPU:0, one launch (start us, length us, event | category | flops | bytes accessed | tf_op | source)
XLA Modules:
  0.0 74.8 jit_solution(2239254070190780521)
XLA Ops:
  0.0 0.0 copy-start.2
  0.0 1.2 %copy.23 = bf16[256,2,640]{2,0,1:T(8,128)(2,1)S(1)} copy(bf16[256,2,640]{2,1,0:T(2,128)(2,1)} %param.5) | data formatting | bytes 1310720 | tf_op args[1]
  1.2 0.1 copy.18
  1.3 1.1 %copy.19 = bf16[640,512]{1,0:T(8,128)(2,1)} copy(bf16[640,512]{0,1:T(8,128)(2,1)S(1)} %bitcast.13) | data formatting | bytes 1310720 | tf_op jit(solution)/shard_map/optimization_barrier | solution.py:304
  2.4 7.3 %all-to-all-start = ((bf16[8,80,512]{2,1,0:T(8,128)(2,1)}), bf16[8,80,512]{2,1,0:T(8,128)(2,1)S(1)}, u32[]{:S(2)}, u32[]{:S(2)}) async-start(bf16[8,80,512]{2,1,0:T(8,128)(2,1)} %bitcast.3), calls=%async_computation | async-start | bytes 1310720 | tf_op jit(solution)/shard_map/all_to_all | solution.py:299
  9.7 0.8 %reshape.19 = bf16[32,8,2,4]{1,0,3,2:T(8,128)(2,1)S(1)} reshape(bf16[256,2,4]{0,2,1:T(4,128)(2,1)} %param.4) | data formatting | bytes 8192 | tf_op jit(solution)/shard_map/reshape | solution.py:283
  10.5 0.1 copy.20
  10.6 0.1 broadcast_in_dim_reshape.3
  10.7 2.9 %collective-permute-start = (bf16[1,4,512]{2,1,0:T(4,128)(2,1)S(1)}, bf16[1,4,512]{2,1,0:T(4,128)(2,1)S(1)}, u32[]{:S(2)}, u32[]{:S(2)}) collective-permute-start(bf16[1,4,512]{2,1,0:T(4,128)(2,1)S(1)} %broadcast_in_dim_reshape.3), channel_id=1, source_target_pairs={{0,4},{1,5},{2,6},{3,7},{4,0},{5,1},{6,2},{7,3},{8,12},{9,13},{10,... | collective-permute-start | bytes 12296 | tf_op jit(solution)/shard_map/ppermute | solution.py:290
  13.6 13.6 %collective-permute-done = bf16[1,4,512]{2,1,0:T(4,128)(2,1)S(1)} collective-permute-done((bf16[1,4,512]{2,1,0:T(4,128)(2,1)S(1)}, bf16[1,4,512]{2,1,0:T(4,128)(2,1)S(1)}, u32[]{:S(2)}, u32[]{:S(2)}) %collective-permute-start) | collective-permute-done | bytes 4128 | tf_op jit(solution)/shard_map/ppermute | solution.py:290
  27.2 1.5 %collective-permute-start.1 = (bf16[2,4,512]{2,1,0:T(4,128)(2,1)S(1)}, bf16[2,4,512]{2,1,0:T(4,128)(2,1)S(1)}, u32[]{:S(2)}, u32[]{:S(2)}) collective-permute-start(bf16[2,4,512]{2,1,0:T(4,128)(2,1)S(1)} %maximum_select_fusion.4), channel_id=1, source_target_pairs={{0,1},{1,0},{2,3},{3,2},{4,5},{5,4},{6,7},{7,6},{8,9},{9,8},{10,11... | collective-permute-start | bytes 24584 | tf_op jit(solution)/shard_map/ppermute | solution.py:290
  28.7 2.2 %collective-permute-done.1 = bf16[2,4,512]{2,1,0:T(4,128)(2,1)S(1)} collective-permute-done((bf16[2,4,512]{2,1,0:T(4,128)(2,1)S(1)}, bf16[2,4,512]{2,1,0:T(4,128)(2,1)S(1)}, u32[]{:S(2)}, u32[]{:S(2)}) %collective-permute-start.1) | collective-permute-done | bytes 8224 | tf_op jit(solution)/shard_map/ppermute | solution.py:290
  30.9 0.1 collective-permute-start.2
  31.0 3.7 %collective-permute-done.2 = bf16[4,4,512]{2,1,0:T(4,128)(2,1)S(1)} collective-permute-done((bf16[4,4,512]{2,1,0:T(4,128)(2,1)S(1)}, bf16[4,4,512]{2,1,0:T(4,128)(2,1)S(1)}, u32[]{:S(2)}, u32[]{:S(2)}) %collective-permute-start.2) | collective-permute-done | bytes 16416 | tf_op jit(solution)/shard_map/ppermute | solution.py:290
  34.8 0.1 collective-permute-start.3
  34.8 1.2 %collective-permute-done.3 = bf16[8,4,512]{2,1,0:T(4,128)(2,1)S(1)} collective-permute-done((bf16[8,4,512]{2,1,0:T(4,128)(2,1)S(1)}, bf16[8,4,512]{2,1,0:T(4,128)(2,1)S(1)}, u32[]{:S(2)}, u32[]{:S(2)}) %collective-permute-start.3) | collective-permute-done | bytes 32800 | tf_op jit(solution)/shard_map/ppermute | solution.py:290
  36.0 0.1 maximum_select_fusion.1
  36.1 1.6 %collective-permute-start.4 = (bf16[8,8,512]{2,1,0:T(8,128)(2,1)S(1)}, bf16[8,8,512]{2,1,0:T(8,128)(2,1)S(1)}, u32[]{:S(2)}, u32[]{:S(2)}) collective-permute-start(bf16[8,8,512]{2,1,0:T(8,128)(2,1)S(1)} %maximum_select_fusion.1), channel_id=1, source_target_pairs={{0,16},{8,24},{16,0},{24,8},{1,17},{9,25},{17,1},{25,9},{2,18},{10... | collective-permute-start | bytes 196616 | tf_op jit(solution)/shard_map/ppermute | solution.py:290
  37.7 0.0 copy-start.1
  37.7 0.9 %copy-done.1 = f32[40,2,512]{2,1,0:T(2,128)S(1)} copy-done((f32[40,2,512]{2,1,0:T(2,128)S(1)}, f32[40,2,512]{2,1,0:T(2,128)}, u32[]{:S(2)}) %copy-start.1) | copy-done | bytes 163864
  38.6 2.0 %table.1.refs_3_ = bf16[2,8,4,512,128]{4,3,2,1,0:T(8,128)(2,1)S(1)} custom-call(f32[40,2,512]{2,1,0:T(2,128)S(1)} %copy-done.1), custom_call_target="tpu_custom_call" | custom-call | tf_op jit(solution)/shard_map/table/pallas_call | solution.py:64
  40.6 0.0 copy-start
  40.6 3.2 %copy-done = bf16[2,8,4,512,128]{4,3,2,1,0:T(8,128)(2,1)} copy-done((bf16[2,8,4,512,128]{4,3,2,1,0:T(8,128)(2,1)}, bf16[2,8,4,512,128]{4,3,2,1,0:T(8,128)(2,1)S(1)}, u32[]{:S(2)}) %copy-start) | copy-done | bytes 8388632
  43.8 0.0 collective-permute-done.4
  43.8 0.0 all-to-all-done.refs_1_
  43.8 0.0 copy-done.2
  43.9 19.9 %transform.1 = f32[16,80]{1,0:T(8,128)S(1)} custom-call(s32[16]{0:T(128)S(1)} %copy-done.2, bf16[8,80,512]{2,1,0:T(8,128)(2,1)S(1)} %all-to-all-done.refs_1_, bf16[8,16,512]{2,1,0:T(8,128)(2,1)S(1)} %maximum_select_fusion.refs_2_, bf16[2,8,4,512,128]{4,3,2,1,0:T(8,128)(2,1)} %copy-done), custom_call_target="tpu_custom_call" | custom-call | tf_op jit(solution)/shard_map/transform/pallas_call | solution.py:257
  63.8 10.3 %all_to_all.10 = f32[8,16,80]{2,1,0:T(8,128)S(1)} all-to-all(f32[8,16,80]{2,1,0:T(8,128)S(1)} %broadcast_in_dim.2), channel_id=1, replica_groups=mesh['group'=4,'freq'=8] {'freq'}, dimensions={0} | all-to-all | bytes 81920 | tf_op jit(solution)/shard_map/all_to_all | solution.py:299
  74.1 0.7 reshape.20
  (6 shorter events, 0.1 us)
Async XLA Ops:
  0.0 43.8 %copy-start.2 = (s32[16]{0:T(128)S(1)}, s32[16]{0:T(128)}, u32[]{:S(2)}) copy-start(s32[16]{0:T(128)} %refs_0_.1) | copy-start | bytes 196
  2.4 41.4 %all-to-all-start = ((bf16[8,80,512]{2,1,0:T(8,128)(2,1)}), bf16[8,80,512]{2,1,0:T(8,128)(2,1)S(1)}, u32[]{:S(2)}, u32[]{:S(2)}) async-start(bf16[8,80,512]{2,1,0:T(8,128)(2,1)} %bitcast.3), calls=%async_computation | async-start | bytes 1310720 | tf_op jit(solution)/shard_map/all_to_all | solution.py:299
  10.7 16.5 %collective-permute-start = (bf16[1,4,512]{2,1,0:T(4,128)(2,1)S(1)}, bf16[1,4,512]{2,1,0:T(4,128)(2,1)S(1)}, u32[]{:S(2)}, u32[]{:S(2)}) collective-permute-start(bf16[1,4,512]{2,1,0:T(4,128)(2,1)S(1)} %broadcast_in_dim_reshape.3), channel_id=1, source_target_pairs={{0,4},{1,5},{2,6},{3,7},{4,0},{5,1},{6,2},{7,3},{8,12},{9,13},{10,... | collective-permute-start | bytes 12296 | tf_op jit(solution)/shard_map/ppermute | solution.py:290
  27.2 3.7 %collective-permute-start.1 = (bf16[2,4,512]{2,1,0:T(4,128)(2,1)S(1)}, bf16[2,4,512]{2,1,0:T(4,128)(2,1)S(1)}, u32[]{:S(2)}, u32[]{:S(2)}) collective-permute-start(bf16[2,4,512]{2,1,0:T(4,128)(2,1)S(1)} %maximum_select_fusion.4), channel_id=1, source_target_pairs={{0,1},{1,0},{2,3},{3,2},{4,5},{5,4},{6,7},{7,6},{8,9},{9,8},{10,11... | collective-permute-start | bytes 24584 | tf_op jit(solution)/shard_map/ppermute | solution.py:290
  30.9 3.8 %collective-permute-start.2 = (bf16[4,4,512]{2,1,0:T(4,128)(2,1)S(1)}, bf16[4,4,512]{2,1,0:T(4,128)(2,1)S(1)}, u32[]{:S(2)}, u32[]{:S(2)}) collective-permute-start(bf16[4,4,512]{2,1,0:T(4,128)(2,1)S(1)} %maximum_select_fusion.3), channel_id=1, source_target_pairs={{0,2},{1,3},{2,0},{3,1},{4,6},{5,7},{6,4},{7,5},{8,10},{9,11},{10,... | collective-permute-start | bytes 49160 | tf_op jit(solution)/shard_map/ppermute | solution.py:290
  34.8 1.3 %collective-permute-start.3 = (bf16[8,4,512]{2,1,0:T(4,128)(2,1)S(1)}, bf16[8,4,512]{2,1,0:T(4,128)(2,1)S(1)}, u32[]{:S(2)}, u32[]{:S(2)}) collective-permute-start(bf16[8,4,512]{2,1,0:T(4,128)(2,1)S(1)} %maximum_select_fusion.2), channel_id=1, source_target_pairs={{0,8},{8,0},{16,24},{24,16},{1,9},{9,1},{17,25},{25,17},{2,10},{10... | collective-permute-start | bytes 98312 | tf_op jit(solution)/shard_map/ppermute | solution.py:290
  36.1 7.7 %collective-permute-start.4 = (bf16[8,8,512]{2,1,0:T(8,128)(2,1)S(1)}, bf16[8,8,512]{2,1,0:T(8,128)(2,1)S(1)}, u32[]{:S(2)}, u32[]{:S(2)}) collective-permute-start(bf16[8,8,512]{2,1,0:T(8,128)(2,1)S(1)} %maximum_select_fusion.1), channel_id=1, source_target_pairs={{0,16},{8,24},{16,0},{24,8},{1,17},{9,25},{17,1},{25,9},{2,18},{10... | collective-permute-start | bytes 196616 | tf_op jit(solution)/shard_map/ppermute | solution.py:290
  37.7 0.9 %copy-start.1 = (f32[40,2,512]{2,1,0:T(2,128)S(1)}, f32[40,2,512]{2,1,0:T(2,128)}, u32[]{:S(2)}) copy-start(f32[40,2,512]{2,1,0:T(2,128)} %constant.16.clone.factor_ref) | copy-start | bytes 491524
  40.6 3.2 %copy-start = (bf16[2,8,4,512,128]{4,3,2,1,0:T(8,128)(2,1)}, bf16[2,8,4,512,128]{4,3,2,1,0:T(8,128)(2,1)S(1)}, u32[]{:S(2)}) copy-start(bf16[2,8,4,512,128]{4,3,2,1,0:T(8,128)(2,1)S(1)} %table.1.refs_3_) | copy-start | bytes 25165828
